TPU v7x, 32 devices: a 4x4x1 block of a 4x4x8 slice. The times are simulated.
32 devices in a mesh: dp: 1 (over z), tp: 4 (over y), sp: 8 (over x, core).
Axes of the slice: x: 4, y: 4, z: 1, core: 2. Of those that a mesh axis runs over, the one named last changes fastest.
The devices are a block of a 4x4x8 slice.
Arguments:
- hidden: bfloat16 [256, 6144], P('dp')
- lengths: int32 [256], P('dp')
- k_cache: bfloat16 [256, 256, 8, 128], P('dp', 'sp', 'tp')
- v_cache: bfloat16 [256, 256, 8, 128], P('dp', 'sp', 'tp')
- norm_gain: bfloat16 [6144], replicated
- w_query: bfloat16 [6144, 6144], P(None, 'tp')
- w_key: bfloat16 [6144, 1024], P(None, 'tp')
- w_value: bfloat16 [6144, 1024], P(None, 'tp')
- w_out: bfloat16 [6144, 6144], P('tp')
Outputs:
- output 1: bfloat16 [256, 6144], P('dp')
- output 2: bfloat16 [256, 256, 8, 128], P('dp', 'sp', 'tp')
- output 3: bfloat16 [256, 256, 8, 128], P('dp', 'sp', 'tp')
All inputs are finite; a program needn't handle non-finite values.
Results may differ from a plain program's by a relative error of at most 0.00455691.
Values sent between devices are 32-bit elements.
A program may use at most 768 MiB of HBM per device.

v0:
```python
import jax
import jax.numpy as jnp
from jax import lax
from jax.sharding import PartitionSpec as P

EPS = 1e-6
NEG_BIG = -1e30


def solution(mesh):
    cache_spec = P('dp', 'sp', 'tp', None)

    def local_step(hidden, lengths, k_cache, v_cache, norm_gain, w_query, w_key, w_value, w_out):
        batch, seq_block, kv_local, head_dim = k_cache.shape
        heads_local = w_query.shape[1] // head_dim
        group = heads_local // kv_local
        hid_f32 = hidden.astype(jnp.float32)
        inv_rms = lax.rsqrt(jnp.mean(hid_f32 * hid_f32, axis=-1, keepdims=True) + EPS)
        normed = (hid_f32 * inv_rms * norm_gain.astype(jnp.float32)).astype(jnp.bfloat16)
        query = jnp.dot(normed, w_query, preferred_element_type=jnp.float32).astype(jnp.bfloat16)
        query = query.reshape(batch, kv_local, group, head_dim)
        new_key = jnp.dot(normed, w_key, preferred_element_type=jnp.float32).astype(jnp.bfloat16)
        new_value = jnp.dot(normed, w_value, preferred_element_type=jnp.float32).astype(jnp.bfloat16)
        positions = lax.axis_index('sp') * seq_block + jnp.arange(seq_block)
        at_slot = (positions[None, :] == lengths[:, None])[:, :, None, None]
        k_new = jnp.where(at_slot, new_key.reshape(batch, 1, kv_local, head_dim), k_cache)
        v_new = jnp.where(at_slot, new_value.reshape(batch, 1, kv_local, head_dim), v_cache)
        scores = jnp.einsum('bkgd,btkd->bkgt', query, k_new, preferred_element_type=jnp.float32) * (head_dim ** -0.5)
        valid = (positions[None, :] <= lengths[:, None])[:, None, None, :]
        scores = jnp.where(valid, scores, NEG_BIG)
        local_peak = jnp.max(scores, axis=-1, keepdims=True)
        exp_vals = jnp.where(valid, jnp.exp(scores - local_peak), 0.0)
        local_denom = jnp.sum(exp_vals, axis=-1, keepdims=True)
        local_acc = jnp.einsum('bkgt,btkd->bkgd', exp_vals.astype(jnp.bfloat16), v_new, preferred_element_type=jnp.float32)
        global_peak = lax.pmax(local_peak, 'sp')
        rescale = jnp.exp(local_peak - global_peak)
        total_acc, total_denom = lax.psum((local_acc * rescale, local_denom * rescale), 'sp')
        attn_out = (total_acc / total_denom).astype(jnp.bfloat16).reshape(batch, heads_local * head_dim)
        part_out = jnp.dot(attn_out, w_out, preferred_element_type=jnp.float32)
        head_sum = lax.psum(part_out, 'tp')
        hidden_out = (hid_f32 + head_sum).astype(jnp.bfloat16)
        return hidden_out, k_new, v_new

    return jax.shard_map(
        local_step,
        mesh=mesh,
        in_specs=(P('dp', None), P('dp'), cache_spec, cache_spec, P(None), P(None, 'tp'), P(None, 'tp'), P(None, 'tp'), P('tp', None)),
        out_specs=(P('dp', None), cache_spec, cache_spec),
        check_vma=False,
    )
```

profile of v0, /device:TPU:97, one launch (start us, length us, event | category | flops | bytes accessed | tf_op | source)
XLA Modules:
  0.0 295.4 jit_solution(2088722438509653783)
XLA Ops:
  7.2 0.0 copy-start
  7.2 0.0 copy-start.6
  7.2 0.1 all-reduce.3.cloned.1.call-start
  7.3 0.0 copy-start.3
  7.3 2.7 fusion
  10.1 0.0 copy-done.6
  10.1 0.0 copy-done
  10.1 0.9 copy-done.3
  11.0 0.0 copy-start.5
  11.0 1.7 convolution_convert_fusion.2
  12.7 0.0 copy-done.5
  12.7 0.1 copy.17
  12.9 0.0 copy-start.4
  12.9 4.6 %convolution_convert_fusion.1 = bf16[256,256]{0,1:T(8,128)(2,1)S(1)} fusion(bf16[6144,256]{1,0:T(8,128)(2,1)} %param.16, bf16[256,6144]{1,0:T(8,128)(2,1)} %param.9, f32[6144]{0:T(1024)} %copy-done.5, f32[256]{0:T(256)S(1)} %add_rsqrt_fusion), kind=kOutput, calls=%fused_computation.21 | convolution fusion | flops 811663360 | bytes 6448128 | tf_op jit(solution)/shard_map/dot_general | solution.py:23
  17.5 0.1 copy.20
  17.6 0.0 copy-done.4
  17.7 10.0 %convolution_convert_fusion = bf16[256,1536]{1,0:T(8,128)(2,1)} fusion(bf16[6144,1536]{1,0:T(8,128)(2,1)} %param.14, bf16[256,6144]{1,0:T(8,128)(2,1)S(1)} %copy-done.4, f32[6144]{0:T(1024)} %copy-done.5, f32[256]{0:T(256)S(1)} %add_rsqrt_fusion), kind=kOutput, calls=%fused_computation.13 | convolution fusion | flops 4838522880 | bytes 22832128 | tf_op jit(solution)/shard_map/dot_general | solution.py:20
  27.7 0.0 copy-start.7
  27.7 1.4 copy.16
  29.1 1.0 copy.18
  30.1 0.0 copy-done.7
  30.1 0.1 broadcast_compare_fusion.1
  30.3 13.8 %broadcast_select_fusion.1 = (bf16[256,32,2,128]{3,2,1,0:T(2,128)(2,1)S(1)}, bf16[256,32,2,128]{3,2,1,0:T(2,128)(2,1)}) fusion(bf16[256,32,2,128]{3,2,1,0:T(2,128)(2,1)} %param.11, pred[256,32]{1,0:T(8,128)(4,1)S(1)} %get-tuple-element.8, bf16[256,2,128]{2,1,0:T(2,128)(2,1)S(1)} %copy.17, bf16[256,32,2,128]{3,2,1,0:T(2,128)(2,1)} %param.12, ...), kind=kLoop, calls=%fused_computation.4 | loop fusion | flops 4194304 | bytes 17047552 | tf_op jit(solution)/shard_map/jit(_where)/select_n | solution.py:26
  44.0 0.0 copy-start.2
  44.1 2.8 fusion.8
  46.8 0.0 copy-done.2
  46.8 26.9 %pmax.7 = f32[256,2,6,1]{2,1,0,3:T(2,128)S(1)} all-reduce(f32[256,2,6,1]{2,1,0,3:T(2,128)S(1)} %bitcast.21), channel_id=1, replica_groups=mesh['dp'=1,'tp'=4,'sp'=8] {'sp'}, use_global_device_ids=true, to_apply=%region_2.3 | all-reduce | flops 3072 | bytes 24576 | tf_op jit(solution)/shard_map/pmax | solution.py:35
  73.8 1.6 fusion.12
  75.4 0.3 fusion.20
  75.7 4.2 %fusion.9 = f32[256,2,6,128]{3,2,1,0:T(8,128)} fusion(bf16[256,32,2,128]{3,2,1,0:T(2,128)(2,1)} %get-tuple-element.6, f32[256,2,6,32]{3,2,1,0:T(8,128)S(1)} %get-tuple-element.10, f32[256,2,6]{2,1,0:T(2,128)S(1)} %get-tuple-element.4, f32[256,2,6]{2,1,0:T(2,128)S(1)} %get-tuple-element.9, pred[256,32]{1,0:T(8,128)(4,1)S(1)} %get-tuple-element.7), kind=kOutput, calls=%fused_computation.18 | convolution fusion | flops 26050560 | bytes 6193152 | tf_op jit(solution)/shard_map/bkgt,btkd->bkgd/dot_general | solution.py:34
  79.9 0.1 all-reduce.3.cloned.1.call-update
  79.9 0.1 all-reduce.5.cloned.1.call-start
  80.0 28.0 %psum.22 = f32[256,2,6]{2,1,0:T(2,128)S(1)} all-reduce(f32[256,2,6]{2,1,0:T(2,128)S(1)} %get-tuple-element.3), channel_id=1, replica_groups=mesh['dp'=1,'tp'=4,'sp'=8] {'sp'}, use_global_device_ids=true, to_apply=%region_5.6 | all-reduce | flops 3072 | bytes 24576 | tf_op jit(solution)/shard_map/psum | solution.py:37
  108.0 35.0 %all-reduce.3.cloned.1.call-done = f32[256,2,6,128]{3,2,1,0:T(8,128)} async-done(((f32[256,2,6,128]{3,2,1,0:T(8,128)}), f32[256,2,6,128]{3,2,1,0:T(8,128)}) %all-reduce.3.cloned.1.call-update) | async-done | bytes 1572880 | tf_op jit(solution)/shard_map/psum | solution.py:37
  143.0 1.9 divide_convert_fusion
  145.0 0.7 copy.22
  145.7 13.5 %fusion.28 = f32[256,6144]{1,0:T(8,128)} fusion(bf16[256,1536]{0,1:T(8,128)(2,1)S(1)} %bitcast.22, bf16[1536,6144]{1,0:T(8,128)(2,1)} %param.17), kind=kOutput, calls=%fused_computation.39 | convolution fusion | flops 4831838208 | bytes 25952256 | tf_op jit(solution)/shard_map/dot_general | solution.py:39
  159.2 0.1 all-reduce.5.cloned.1.call-update
  159.2 123.0 %all-reduce.5.cloned.1.call-done = f32[256,6144]{1,0:T(8,128)} async-done(((f32[256,6144]{1,0:T(8,128)}), f32[256,6144]{1,0:T(8,128)}) %all-reduce.5.cloned.1.call-update) | async-done | bytes 6291472 | tf_op jit(solution)/shard_map/psum | solution.py:40
  282.2 0.0 copy-start.1
  282.2 6.4 %fusion.3 = bf16[256,6144]{1,0:T(8,128)(2,1)} fusion(f32[256,6144]{1,0:T(8,128)} %all-reduce.5.cloned.1.call-done, bf16[256,6144]{1,0:T(8,128)(2,1)} %param.9), kind=kLoop, calls=%fused_computation.8 | loop fusion | flops 4718592 | bytes 12582912 | tf_op jit(solution)/shard_map/convert_element_type | solution.py:41
  288.6 0.0 copy-done.1
  (3 shorter events, 0.0 us)
Async XLA Ops:
  7.2 2.9 copy-start
  7.2 2.9 copy-start.6
  7.2 135.8 %all-reduce.3.cloned.1.call-start = ((), (), s32[]{:S(2)}) async-start(), calls=%async_computation | async-start | bytes 4194304 | tf_op jit(solution)/shard_map/psum | solution.py:37
  7.3 3.7 %copy-start.3 = (bf16[256,6144]{1,0:T(8,128)(2,1)S(1)}, bf16[256,6144]{1,0:T(8,128)(2,1)}, u32[]{:S(2)}) copy-start(bf16[256,6144]{1,0:T(8,128)(2,1)} %param.9) | copy-start | bytes 9437188
  11.0 1.7 copy-start.5
  12.9 4.8 %copy-start.4 = (bf16[256,6144]{1,0:T(8,128)(2,1)S(1)}, bf16[256,6144]{1,0:T(8,128)(2,1)}, u32[]{:S(2)}) copy-start(bf16[256,6144]{1,0:T(8,128)(2,1)} %param.9) | copy-start | bytes 9437188
  27.7 2.5 copy-start.7
  44.0 2.8 copy-start.2
  79.9 202.3 %all-reduce.5.cloned.1.call-start = ((), (), s32[]{:S(2)}) async-start(), calls=%async_computation.1 | async-start | bytes 12582912 | tf_op jit(solution)/shard_map/psum | solution.py:40
  282.2 6.4 %copy-start.1 = (bf16[6144,256]{1,0:T(8,128)(2,1)S(1)}, bf16[6144,256]{1,0:T(8,128)(2,1)}, u32[]{:S(2)}) copy-start(bf16[6144,256]{1,0:T(8,128)(2,1)} %param.15) | copy-start | bytes 9437188
Sparse Core Ops, SparseCore 0:
  80.1 62.8 all-reduce.2
  159.4 122.8 all-reduce.4
where the time goes:
time: 296 us; the launch traced here: 295 us
  waiting for transfers between devices  158 us (53%)
  blocking collectives  54.9 us (19%)
  matrix products  36.9 us (12%)
  other arithmetic  26.8 us (9%)
  between operations  14.3 us (5%)
  local copies, waits for them, and re-layouts  4.37 us (1%)
    psum x1, waiting for transfers between devices, local_step(): head_sum = lax.psum(part_out, 'tp')  123 us
    psum x1, waiting for transfers between devices, local_step(): lax.psum((local_acc * rescale, local_denom * rescale), 'sp')  35 us
    psum x1, blocking collectives, local_step(): lax.psum((local_acc * rescale, local_denom * rescale), 'sp')  28 us
    pmax x1, blocking collectives, local_step(): global_peak = lax.pmax(local_peak, 'sp')  26.9 us
    select_n x1, other arithmetic, local_step(): jnp.where(at_slot, new_key.reshape(batch, 1, kv_local, head_dim), k_cache)  13.8 us
    dot_general x1, matrix products, local_step(): part_out = jnp.dot(attn_out, w_out, preferred_element_type=jnp.float32)  13.5 us
    dot_general x1, matrix products, local_step(): jnp.dot(normed, w_query, preferred_element_type=jnp.float32)  10 us
    convert_element_type x1, other arithmetic, local_step(): hidden_out = (hid_f32 + head_sum).astype(jnp.bfloat16)  6.35 us
  transfers between devices with their start and end apart: 2, of which 2 were waited for; matrix products, arithmetic and copies ran while one was open for 0% of the time, Pallas kernels for 0%

commit v1 on v0

v1 whole, which is shorter than its diff:
```python
import functools
import math

import jax
import jax.numpy as jnp
from jax import lax
from jax.experimental import pallas as pl
from jax.experimental.pallas import tpu as pltpu
from jax.sharding import PartitionSpec as P

EPS = 1e-6
NEG_BIG = -1e30
MESH = pl.DeviceIdType.MESH
F32 = jnp.float32
BF16 = jnp.bfloat16
MIB = 1 << 20


def attention_kernel(dims, len_ref, hid_hbm, gain_ref, wq_hbm, wk_hbm, wv_hbm, kc_hbm, vc_hbm,
                     acc_ref, kout_hbm, vout_hbm,
                     hbuf, nbuf, wbuf, kbuf, vbuf, qs, ks, vs,
                     sem_h, sem_w, sem_k, sem_v, sem_ko, sem_vo):
    batch, d_model, heads, kv, group, head_dim, seq_block, sp = dims
    n_wq = wq_hbm.shape[1] // 256
    n_w = n_wq + 2
    base = lax.axis_index('sp') * seq_block
    chunk = batch // sp
    rows_h = batch // 4

    hid_copies = [pltpu.make_async_copy(hid_hbm.at[pl.ds(i * rows_h, rows_h)], hbuf.at[pl.ds(i * rows_h, rows_h)], sem_h.at[i])
                  for i in range(4)]
    w_copies = [pltpu.make_async_copy(wq_hbm.at[:, pl.ds(j * 256, 256)], wbuf.at[j], sem_w.at[j]) for j in range(n_wq)]
    w_copies.append(pltpu.make_async_copy(wk_hbm, wbuf.at[n_wq], sem_w.at[n_wq]))
    w_copies.append(pltpu.make_async_copy(wv_hbm, wbuf.at[n_wq + 1], sem_w.at[n_wq + 1]))
    crow = chunk * seq_block

    def cache_copy(c, src, buf, sem):
        return pltpu.make_async_copy(src.at[pl.ds(c * crow, crow)], buf.at[pl.ds(c * crow, crow)], sem.at[c])

    def cache_back(c, buf, dst, sem):
        return pltpu.make_async_copy(buf.at[pl.ds(c * crow, crow)], dst.at[pl.ds(c * crow, crow)], sem.at[c])

    for cp in hid_copies:
        cp.start()
    for cp in w_copies:
        cp.start()
    for c in range(sp):
        cache_copy(c, kc_hbm, kbuf, sem_k).start()
        cache_copy(c, vc_hbm, vbuf, sem_v).start()

    step = 16
    wide = 1024
    for i in range(4):
        hid_copies[i].wait()

        def norm_rows(r, carry, i=i):
            row = pl.multiple_of(i * rows_h + r * step, step)
            total = jnp.zeros((step, 1), F32)
            for w in range(d_model // wide):
                x = hbuf[pl.ds(row, step), w * wide:(w + 1) * wide].astype(F32)
                total = total + jnp.sum(x * x, axis=1, keepdims=True)
            inv = lax.rsqrt(total / d_model + EPS)
            for w in range(d_model // wide):
                x = hbuf[pl.ds(row, step), w * wide:(w + 1) * wide].astype(F32)
                g = gain_ref[:, w * wide:(w + 1) * wide].astype(F32)
                nbuf[pl.ds(row, step), w * wide:(w + 1) * wide] = (x * inv * g).astype(BF16)
            return carry

        lax.fori_loop(0, rows_h // step, norm_rows, 0)

    def project_q(j, carry):
        pltpu.make_async_copy(wk_hbm, wbuf.at[j], sem_w.at[j]).wait()
        res = jnp.dot(nbuf[...], wbuf[j], preferred_element_type=F32)
        for i in range(2):
            qs[pl.ds(2 * j + i, batch, stride=heads), :] = res[:, i * head_dim:(i + 1) * head_dim]
        return carry

    lax.fori_loop(0, n_wq, project_q, 0)
    for n, dst in ((n_wq, ks), (n_wq + 1, vs)):
        w_copies[n].wait()
        res = jnp.dot(nbuf[...], wbuf[n], preferred_element_type=F32)
        for i in range(kv):
            dst[pl.ds(i, batch, stride=kv), :] = res[:, i * head_dim:(i + 1) * head_dim]

    gs = 4
    qrows = gs * heads
    krows = gs * seq_block * kv
    row_id = lax.broadcasted_iota(jnp.int32, (qrows, krows), 0)
    col_id = lax.broadcasted_iota(jnp.int32, (qrows, krows), 1)
    same = ((row_id // heads == col_id // (seq_block * kv))
            & ((row_id % heads) // group == col_id % kv))
    col_row = lax.broadcasted_iota(jnp.int32, (1, krows), 1)
    col_seq = col_row // (seq_block * kv)
    col_pos = (col_row % (seq_block * kv)) // kv
    half_rows = chunk * heads // 2
    diag = (lax.broadcasted_iota(jnp.int32, (half_rows, 128), 0) % 128
            == lax.broadcasted_iota(jnp.int32, (half_rows, 128), 1))
    fold = (head_dim ** -0.5) * math.log2(math.e)
    spare = batch * seq_block

    def pack_column(col):
        spread = jnp.where(diag, jnp.broadcast_to(col, (half_rows, 128)), 0.0)
        out = []
        for r in range(0, half_rows, 128):
            out.append(jnp.sum(spread[r:min(r + 128, half_rows)], axis=0, keepdims=True))
        return jnp.concatenate(out, axis=0)

    def attend(c, carry):
        cache_copy(c, kc_hbm, kbuf, sem_k).wait()
        cache_copy(c, vc_hbm, vbuf, sem_v).wait()
        b_first = c * chunk
        for g in range(chunk // gs):
            b0 = b_first + g * gs
            kn = ks[pl.ds(pl.multiple_of(b0 * kv, 8), gs * kv), :].astype(BF16)
            vn = vs[pl.ds(pl.multiple_of(b0 * kv, 8), gs * kv), :].astype(BF16)
            for i in range(gs):
                p = len_ref[b0 + i] - base
                inside = (p >= 0) & (p < seq_block)
                at = jnp.where(inside, (b0 + i) * seq_block + p, spare)
                kbuf[at] = kn[i * kv:(i + 1) * kv]
                vbuf[at] = vn[i * kv:(i + 1) * kv]
        cache_back(c, kbuf, kout_hbm, sem_ko).start()
        cache_back(c, vbuf, vout_hbm, sem_vo).start()
        ms, ls = [], []
        for g in range(chunk // gs):
            b0 = b_first + g * gs
            q = qs[pl.ds(pl.multiple_of(b0 * heads, 8), qrows), :].astype(BF16)
            k = kbuf.at[pl.ds(b0 * seq_block, gs * seq_block)].reshape(krows, head_dim)[...]
            v = vbuf.at[pl.ds(b0 * seq_block, gs * seq_block)].reshape(krows, head_dim)[...]
            s = lax.dot_general(q, k, (((1,), (1,)), ((), ())), preferred_element_type=F32)
            last = jnp.full((1, krows), len_ref[b0] - base, jnp.int32)
            for i in range(1, gs):
                last = jnp.where(col_seq == i, len_ref[b0 + i] - base, last)
            mask = same & (col_pos <= last)
            s = jnp.where(mask, s * fold, NEG_BIG)
            m = jnp.max(s, axis=1, keepdims=True)
            e = jnp.where(mask, jnp.exp2(s - m), 0.0)
            ls.append(jnp.sum(e, axis=1, keepdims=True))
            ms.append(m)
            o = jnp.dot(e.astype(BF16), v, preferred_element_type=F32)
            half, part = divmod(g, chunk // gs // 2)
            acc_ref[2 * c + half, part * qrows:(part + 1) * qrows, :] = o
        per = chunk // gs // 2
        for half in range(2):
            mp = pack_column(jnp.concatenate(ms[half * per:(half + 1) * per], axis=0))
            lp = pack_column(jnp.concatenate(ls[half * per:(half + 1) * per], axis=0))
            acc_ref[2 * c + half, half_rows:half_rows + 8, :] = jnp.concatenate(
                [mp, lp, jnp.zeros((4, 128), F32)], axis=0)
        return carry

    lax.fori_loop(0, sp, attend, 0)
    for c in range(sp):
        cache_back(c, kbuf, kout_hbm, sem_ko).wait()
        cache_back(c, vbuf, vout_hbm, sem_vo).wait()


def exchange_kernel(dims, acc_ref, hid_hbm, wo_hbm, out_ref,
                    pbuf, xsend, xrecv, obuf, lhs, wbuf, ysend, yrecv, hblk, gbuf,
                    sem_w, sem_hid, sem_ps, sem_pr, sem_xs, sem_xr, sem_os, sem_or, sem_ys, sem_yr,
                    sem_fs, sem_fr, sem_ss, sem_sr, sem_ds, sem_dr):
    batch, d_model, heads, kv, group, head_dim, seq_block, sp = dims
    tp_n = lax.axis_size('tp')
    nx, ny = sp // 2, tp_n
    spi = lax.axis_index('sp')
    y = lax.axis_index('tp')
    x, c = spi // 2, spi % 2
    hr = (batch // sp) * heads // 2
    rows = batch // nx
    cols = d_model // (2 * ny)
    hc = cols // 2

    def at_x(d):
        return (x + d) % nx

    def at_y(d):
        return (y + d) % ny

    def to(tp_pos, sp_pos):
        return {'tp': tp_pos, 'sp': sp_pos}

    partner = to(y, x * 2 + 1 - c)

    def x_dev(d):
        return to(y, at_x(d) * 2 + c)

    def y_dev(d):
        return to(at_y(d), spi)

    def remote(src, dst, ssem, rsem, dev):
        return pltpu.make_async_remote_copy(src_ref=src, dst_ref=dst, send_sem=ssem, recv_sem=rsem,
                                            device_id=dev, device_id_type=MESH)

    order = (2, 1, -1, 0)
    w_copies = []
    for k, d in enumerate(order):
        first = pl.multiple_of(c * (d_model // 2) + at_y(d) * cols, 128)
        w_copies.append(pltpu.make_async_copy(wo_hbm.at[:, pl.ds(first, cols)], wbuf.at[k], sem_w.at[k]))
    hid_copy = pltpu.make_async_copy(
        hid_hbm.at[pl.ds(pl.multiple_of(x * rows, rows), rows), pl.ds(pl.multiple_of(c * (d_model // 2) + y * cols, 128), cols)],
        hblk, sem_hid)

    barrier = pltpu.get_barrier_semaphore()
    peers = [partner, x_dev(1), x_dev(-1), y_dev(1), y_dev(-1)]
    for dev in peers:
        pl.semaphore_signal(barrier, inc=1, device_id=dev, device_id_type=MESH)
    for cp in w_copies:
        cp.start()
    hid_copy.start()
    pl.semaphore_wait(barrier, len(peers))

    pair = []
    for k, d in enumerate(order):
        src = acc_ref.at[pl.ds(4 * at_x(d) + 2 * (1 - c), 2)]
        pair.append(remote(src, pbuf.at[k], sem_ps.at[k], sem_pr.at[k], partner))
        pair[-1].start()

    eye = (lax.broadcasted_iota(jnp.int32, (hr, 128), 0) % 128
           == lax.broadcasted_iota(jnp.int32, (hr, 128), 1))
    n_stat = -(-hr // 128)

    def column(stat):
        parts = []
        for i in range(n_stat):
            size = min(128, hr - i * 128)
            parts.append(jnp.broadcast_to(stat[i:i + 1, :], (size, 128)))
        spread = jnp.where(eye, jnp.concatenate(parts, axis=0), 0.0)
        return jnp.sum(spread, axis=1, keepdims=True)

    def stats(ref):
        return ref[hr:hr + n_stat, :], ref[hr + n_stat:hr + 2 * n_stat, :]

    def merge(refs):
        both = [stats(r) for r in refs]
        peak = functools.reduce(jnp.maximum, [m for m, _ in both])
        scale = [jnp.exp2(m - peak) for m, _ in both]
        denom = sum(l * s for (_, l), s in zip(both, scale))
        total = sum(r[0:hr, :] * column(s) for r, s in zip(refs, scale))
        return total, peak, denom

    def merge_into(dst, refs):
        total, peak, denom = merge(refs)
        dst[0:hr, :] = total
        dst[hr:hr + 8, :] = jnp.concatenate([peak, denom, jnp.zeros((8 - 2 * n_stat, 128), F32)], axis=0)

    def mine(d, half):
        return acc_ref.at[4 * at_x(d) + 2 * c + half]

    xc = [remote(xsend.at[i], xrecv.at[i], sem_xs.at[i], sem_xr.at[i], x_dev(1 if i in (0, 2, 4) else -1))
          for i in range(6)]
    pair[0].wait_recv()
    merge_into(xsend.at[0], [mine(2, 0), pbuf.at[0, 0]])
    xc[0].start()
    merge_into(xsend.at[1], [mine(2, 1), pbuf.at[0, 1]])
    xc[1].start()
    pair[1].wait_recv()
    merge_into(xsend.at[2], [mine(1, 1), pbuf.at[1, 1]])
    xc[2].start()
    pair[2].wait_recv()
    merge_into(xsend.at[3], [mine(-1, 0), pbuf.at[2, 0]])
    xc[3].start()
    xc[0].wait_recv()
    merge_into(xsend.at[4], [mine(1, 0), pbuf.at[1, 0], xrecv.at[0]])
    xc[4].start()
    xc[1].wait_recv()
    merge_into(xsend.at[5], [mine(-1, 1), pbuf.at[2, 1], xrecv.at[1]])
    xc[5].start()
    pair[3].wait_recv()
    oc = []
    for half, (near, far) in enumerate(((3, 4), (2, 5))):
        xc[near].wait_recv()
        xc[far].wait_recv()
        total, _, denom = merge([mine(0, half), pbuf.at[3, half], xrecv.at[near], xrecv.at[far]])
        o = total / column(denom)
        obuf[c, half * hr:(half + 1) * hr, :] = o.astype(BF16).astype(F32)
        oc.append(remote(obuf.at[c, pl.ds(half * hr, hr)], obuf.at[c, pl.ds(half * hr, hr)],
                         sem_os.at[half], sem_or.at[half], partner))
        oc[-1].start()
    for cp in oc:
        cp.wait_recv()
    half_seq = rows // 2
    for core in range(2):
        for h in range(heads):
            lhs[core * half_seq:(core + 1) * half_seq, h * head_dim:(h + 1) * head_dim] = (
                obuf[core, pl.ds(h, half_seq, stride=heads), :].astype(BF16))

    yc = [remote(ysend.at[i], yrecv.at[i], sem_ys.at[i], sem_yr.at[i], y_dev(1 if i in (0, 2, 4) else -1))
          for i in range(6)]

    def product(k):
        w_copies[k].wait()
        return jnp.dot(lhs[...], wbuf[k], preferred_element_type=F32)

    far_part = product(0)
    ysend[0] = far_part[:, :hc]
    ysend[1] = far_part[:, hc:]
    yc[0].start()
    yc[1].start()
    right_part = product(1)
    ysend[2] = right_part[:, hc:]
    ysend[4] = right_part[:, :hc]
    yc[2].start()
    left_part = product(2)
    ysend[3] = left_part[:, :hc]
    ysend[5] = left_part[:, hc:]
    yc[3].start()
    yc[0].wait_recv()
    ysend[4] = ysend[4] + yrecv[0]
    yc[4].start()
    yc[1].wait_recv()
    ysend[5] = ysend[5] + yrecv[1]
    yc[5].start()
    own_part = product(3)
    hid_copy.wait()

    f = x + c * (y - x)
    s = y + c * (x - y)

    def f_dev(d):
        return to((y + c * d) % ny, ((x + (1 - c) * d) % nx) * 2 + c)

    def s_dev(d):
        return to((y + (1 - c) * d) % ny, ((x + c * d) % nx) * 2 + c)

    def slot(fd, sd, half):
        return gbuf.at[c, (f + fd) % nx, (s + sd) % ny, half]

    def d2d(fd, sd, half):
        i = ((fd % nx) * ny + (sd % ny)) * 2 + half
        return remote(slot(fd, sd, half), slot(fd, sd, half), sem_ds.at[i], sem_dr.at[i], partner)

    def f_copy(fd, half, direction):
        i = ((fd % nx) * 2 + half) * 2 + (direction > 0)
        return remote(slot(fd, 0, half), slot(fd, 0, half), sem_fs.at[i], sem_fr.at[i], f_dev(direction))

    def f_arrival(fd, half, direction):
        i = (((fd + direction) % nx) * 2 + half) * 2 + (direction > 0)
        return remote(slot(fd, 0, half), slot(fd, 0, half), sem_fs.at[i], sem_fr.at[i], f_dev(direction))

    def s_index(fd, sd, half, direction):
        return (((fd % nx) * ny + (sd % ny)) * 2 + half) * 2 + (direction > 0)

    def s_copy(fd, sd, half, direction):
        i = s_index(fd, sd, half, direction)
        return remote(slot(fd, sd, half), slot(fd, sd, half), sem_ss.at[i], sem_sr.at[i], s_dev(direction))

    started = []

    def go(copy):
        copy.start()
        started.append(copy)

    for half, (near, far) in enumerate(((3, 4), (2, 5))):
        yc[near].wait_recv()
        yc[far].wait_recv()
        mid = own_part[:, half * hc:(half + 1) * hc] + yrecv[near] + yrecv[far]
        val = hblk[:, half * hc:(half + 1) * hc].astype(F32) + mid
        gbuf[c, f, s, half] = val.astype(BF16).astype(F32)
        for direction in (1, -1):
            go(f_copy(0, half, direction))
            go(s_copy(0, 0, half, direction))
        go(d2d(0, 0, half))

    def f_wait(fd, half, direction):
        i = (((fd + direction) % nx) * 2 + half) * 2 + (direction > 0)
        remote(slot(fd, 0, half), slot(fd, 0, half), sem_fs.at[i], sem_fr.at[i], f_dev(direction)).wait_recv()

    def s_wait(fd, sd, half, direction):
        i = s_index(fd, sd + direction, half, direction)
        remote(slot(fd, sd, half), slot(fd, sd, half), sem_ss.at[i], sem_sr.at[i], s_dev(direction)).wait_recv()

    def spread(fd, half):
        for direction in (1, -1):
            go(s_copy(fd, 0, half, direction))
        go(d2d(fd, 0, half))

    def ring(fd):
        for half, sd in ((0, -1), (1, 1)):
            s_wait(fd, sd, half, -sd)
            go(s_copy(fd, sd, half, -sd))
            go(d2d(fd, sd, half))
        for half, sd in ((1, -1), (0, 1)):
            s_wait(fd, sd, half, -sd)
            go(d2d(fd, sd, half))

    def ring_end(fd):
        for half, direction in ((0, 1), (1, -1)):
            s_wait(fd, 2, half, direction)
            go(d2d(fd, 2, half))

    def place(core, fd, sd):
        fi = (f + fd) % nx
        si = (s + sd) % ny
        if core is None:
            xi, yi, ci = fi + c * (si - fi), si + c * (fi - si), c
        else:
            xi, yi, ci = si + c * (fi - si), fi + c * (si - fi), 1 - c
        first = ci * (d_model // 2) + yi * cols
        for half in range(2):
            out_ref[pl.ds(pl.multiple_of(xi * rows, rows), rows),
                    pl.ds(pl.multiple_of(first + half * hc, 128), hc)] = gbuf[ci, fi, si, half].astype(BF16)

    f_wait(-1, 0, 1)
    go(f_copy(-1, 0, 1))
    spread(-1, 0)
    f_wait(1, 1, -1)
    go(f_copy(1, 1, -1))
    spread(1, 1)
    f_wait(-1, 1, 1)
    spread(-1, 1)
    f_wait(1, 0, -1)
    spread(1, 0)
    place(None, 0, 0)
    ring(0)
    place(None, -1, 0)
    place(None, 1, 0)
    f_wait(2, 0, 1)
    spread(2, 0)
    f_wait(2, 1, -1)
    spread(2, 1)
    place(None, 0, -1)
    place(None, 0, 1)
    ring(-1)
    place(None, 2, 0)
    ring(1)
    ring_end(0)
    place(None, -1, -1)
    place(None, -1, 1)
    place(None, 1, -1)
    place(None, 1, 1)
    place(None, 0, 2)
    ring(2)
    ring_end(-1)
    place(None, 2, -1)
    place(None, 2, 1)
    place(None, -1, 2)
    ring_end(1)
    place(None, 1, 2)
    ring_end(2)
    place(None, 2, 2)

    def d2d_wait(fd, sd, half):
        i = ((fd % nx) * ny + (sd % ny)) * 2 + half
        there = gbuf.at[1 - c, (s + fd) % nx, (f + sd) % ny, half]
        remote(there, there, sem_ds.at[i], sem_dr.at[i], partner).wait_recv()

    def place_other(fd, sd):
        fi, si = (s + fd) % nx, (f + sd) % ny
        ci = 1 - c
        xi = si + c * (fi - si)
        yi = fi + c * (si - fi)
        first = ci * (d_model // 2) + yi * cols
        for half in range(2):
            out_ref[pl.ds(pl.multiple_of(xi * rows, rows), rows),
                    pl.ds(pl.multiple_of(first + half * hc, 128), hc)] = gbuf[ci, fi, si, half].astype(BF16)

    for fd, sd in ((0, 0), (-1, 0), (1, 0), (0, -1), (0, 1), (2, 0), (-1, -1), (-1, 1), (1, -1), (1, 1), (0, 2),
                   (2, -1), (2, 1), (-1, 2), (1, 2), (2, 2)):
        for half in range(2):
            d2d_wait(fd, sd, half)
        place_other(fd, sd)

    for cp in pair + xc + oc + yc + started:
        cp.wait_send()


def solution(mesh):
    cache_spec = P('dp', 'sp', 'tp', None)
    sp = mesh.shape['sp']
    tp = mesh.shape['tp']

    def local_step(hidden, lengths, k_cache, v_cache, norm_gain, w_query, w_key, w_value, w_out):
        batch, seq_block, kv, head_dim = k_cache.shape
        d_model = hidden.shape[1]
        heads = w_query.shape[1] // head_dim
        group = heads // kv
        dims = (batch, d_model, heads, kv, group, head_dim, seq_block, sp)
        hr = (batch // sp) * heads // 2
        n_w = w_query.shape[1] // 256 + 2
        flat = batch * seq_block
        anyspec = pl.BlockSpec(memory_space=pl.ANY)
        vspec = pl.BlockSpec(memory_space=pltpu.VMEM)
        dma = pltpu.SemaphoreType.DMA

        acc, k_new, v_new = pl.pallas_call(
            functools.partial(attention_kernel, dims),
            out_shape=(jax.ShapeDtypeStruct((2 * sp, hr + 8, 128), F32),
                       jax.ShapeDtypeStruct((flat, kv, head_dim), BF16),
                       jax.ShapeDtypeStruct((flat, kv, head_dim), BF16)),
            in_specs=[pl.BlockSpec(memory_space=pltpu.SMEM), anyspec, vspec] + [anyspec] * 5,
            out_specs=(vspec, anyspec, anyspec),
            scratch_shapes=[
                pltpu.VMEM((batch, d_model), BF16),
                pltpu.VMEM((batch, d_model), BF16),
                pltpu.VMEM((n_w, d_model, 256), BF16),
                pltpu.VMEM((flat + 8, kv, head_dim), BF16),
                pltpu.VMEM((flat + 8, kv, head_dim), BF16),
                pltpu.VMEM((batch * heads, head_dim), F32),
                pltpu.VMEM((batch * kv, head_dim), F32),
                pltpu.VMEM((batch * kv, head_dim), F32),
                dma((4,)), dma((n_w,)), dma((sp,)), dma((sp,)), dma((sp,)), dma((sp,)),
            ],
            compiler_params=pltpu.CompilerParams(vmem_limit_bytes=50 * MIB),
            name='local_attention',
        )(lengths, hidden, norm_gain.reshape(1, d_model), w_query, w_key, w_value,
          k_cache.reshape(flat, kv, head_dim), v_cache.reshape(flat, kv, head_dim))

        nx = sp // 2
        rows = batch // nx
        cols = d_model // (2 * tp)
        n_blocks = nx * tp
        out = pl.pallas_call(
            functools.partial(exchange_kernel, dims),
            out_shape=jax.ShapeDtypeStruct((batch, d_model), BF16),
            in_specs=[vspec, anyspec, anyspec],
            out_specs=vspec,
            scratch_shapes=[
                pltpu.VMEM((4, 2, hr + 8, 128), F32),
                pltpu.VMEM((6, hr + 8, 128), F32),
                pltpu.VMEM((6, hr + 8, 128), F32),
                pltpu.VMEM((2, 2 * hr, 128), F32),
                pltpu.VMEM((rows, heads * head_dim), BF16),
                pltpu.VMEM((4, heads * head_dim, cols), BF16),
                pltpu.VMEM((6, rows, cols // 2), F32),
                pltpu.VMEM((6, rows, cols // 2), F32),
                pltpu.VMEM((rows, cols), BF16),
                pltpu.VMEM((2, nx, tp, 2, rows, cols // 2), F32),
                dma((4,)), dma, dma((4,)), dma((4,)), dma((6,)), dma((6,)), dma((2,)), dma((2,)), dma((6,)), dma((6,)),
                dma((nx * 4,)), dma((nx * 4,)), dma((n_blocks * 4,)), dma((n_blocks * 4,)),
                dma((n_blocks * 2,)), dma((n_blocks * 2,)),
            ],
            compiler_params=pltpu.CompilerParams(collective_id=0, has_side_effects=True, vmem_limit_bytes=40 * MIB),
            name='exchange',
        )(acc, hidden, w_out)
        return out, k_new.reshape(k_cache.shape), v_new.reshape(v_cache.shape)

    return jax.shard_map(
        local_step,
        mesh=mesh,
        in_specs=(P('dp', None), P('dp'), cache_spec, cache_spec, P(None), P(None, 'tp'), P(None, 'tp'), P(None, 'tp'), P('tp', None)),
        out_specs=(P('dp', None), cache_spec, cache_spec),
        check_vma=False,
    )
```

time: 296 us -> 97.4 us (0.33)
  waiting for transfers between devices: 158 us -> 0 us
  Pallas kernels: 0 us -> 93.5 us
  blocking collectives: 54.9 us -> 0 us
  matrix products: 36.9 us -> 0 us
  other arithmetic: 26.8 us -> 0 us
  between operations: 14.3 us -> 0.67 us
    psum x2 -> x0, waiting for transfers between devices: 158 us -> none  [the longest x1 123 us: local_step(): head_sum = lax.psum(part_out, 'tp')]
    pallas_call x0 -> x2, Pallas kernels: none -> 93.5 us  [the longest x1 51.3 us: local_step(): pl.pallas_call(functools.partial(exchange_kernel, dims), out_shape=jax.Sh...]
    dot_general x6 -> x0, matrix products: 36.9 us -> none  [the longest x1 13.5 us: local_step(): part_out = jnp.dot(attn_out, w_out, preferred_element_type=jnp.float32)]
    psum x1 -> x0, blocking collectives: 28 us -> none  [local_step(): lax.psum((local_acc * rescale, local_denom * rescale), 'sp')]
    pmax x1 -> x0, blocking collectives: 26.9 us -> none  [local_step(): global_peak = lax.pmax(local_peak, 'sp')]
    select_n x1 -> x0, other arithmetic: 13.8 us -> none  [local_step(): jnp.where(at_slot, new_key.reshape(batch, 1, kv_local, head_dim), k_cache)]
    convert_element_type x3 -> x0, other arithmetic: 8.3 us -> none  [the longest x1 6.35 us: local_step(): hidden_out = (hid_f32 + head_sum).astype(jnp.bfloat16)]
    reduce_sum x2 -> x0, other arithmetic: 4.34 us -> none  [the longest x1 2.74 us: local_step(): jnp.mean(hid_f32 * hid_f32, axis=-1, keepdims=True) + EPS]
  transfers between devices with their start and end apart: 2 -> 0, of which waited for: 2 -> 0; matrix products, arithmetic and copies ran while one was open for 0% -> 0% of each run, Pallas kernels for 0% -> 0%
where the time goes in v1:
time: 97.4 us; the launch traced here: 97.2 us
  Pallas kernels  93.5 us (96%)
  local copies, waits for them, and re-layouts  3.07 us (3%)
    pallas_call x1, Pallas kernels, local_step(): pl.pallas_call(functools.partial(exchange_kernel, dims), out_shape=jax.Sh...  51.3 us
    pallas_call x1, Pallas kernels, local_step(): pl.pallas_call(functools.partial(attention_kernel, dims), out_shape=(jax....  42.2 us
    unnamed x5, local copies, waits for them, and re-layouts  2.34 us

profile of v1, /device:TPU:97, one launch (start us, length us, event | category | flops | bytes accessed | tf_op | source)
XLA Modules:
  0.0 97.2 jit_solution(12693737989374960366)
XLA Ops:
  0.6 0.7 reshape.21.gain_ref
  1.4 0.0 copy-start.1
  1.4 0.7 copy-done.1
  2.0 0.0 copy-start
  2.0 42.2 %local_attention.1 = (f32[16,200,128]{2,1,0:T(8,128)S(1)}, bf16[8192,2,128]{2,1,0:T(2,128)(2,1)}, bf16[8192,2,128]{2,1,0:T(2,128)(2,1)}) custom-call(s32[256]{0:T(256)S(1)} %copy-done.1, bf16[256,6144]{1,0:T(8,128)(2,1)} %hid_hbm.3, bf16[1,6144]{1,0:T(2,128)(2,1)S(1)} %reshape.21.gain_ref, bf16[6144,1536]{1,0:T(8,128)(2,1)} %wq_hbm.1, ...), custom_call_target="tpu_custom_call" | custom-call | tf_op jit(solution)/shard_map/local_attention/pallas_call | solution.py:484
  44.2 0.0 copy-done
  44.2 51.3 %exchange.1 = bf16[256,6144]{1,0:T(8,128)(2,1)S(1)} custom-call(f32[16,200,128]{2,1,0:T(8,128)S(1)} %get-tuple-element.6.acc_ref, bf16[256,6144]{1,0:T(8,128)(2,1)S(1)} %copy-done, bf16[1536,6144]{1,0:T(8,128)(2,1)} %wo_hbm.1), custom_call_target="tpu_custom_call" | custom-call | tf_op jit(solution)/shard_map/exchange/pallas_call | solution.py:511
  95.5 1.7 %copy.13 = bf16[256,6144]{1,0:T(8,128)(2,1)} copy(bf16[256,6144]{1,0:T(8,128)(2,1)S(1)} %exchange.1) | data formatting | bytes 6291456
Async XLA Ops:
  1.4 0.7 copy-start.1
  2.0 42.2 %copy-start = (bf16[256,6144]{1,0:T(8,128)(2,1)S(1)}, bf16[256,6144]{1,0:T(8,128)(2,1)}, u32[]{:S(2)}) copy-start(bf16[256,6144]{1,0:T(8,128)(2,1)} %hid_hbm.3) | copy-start | bytes 9437188

commit v2 on v0

v2 whole, which is shorter than its diff:
```python
import functools
import math

import jax
import jax.numpy as jnp
from jax import lax
from jax.experimental import pallas as pl
from jax.experimental.pallas import tpu as pltpu
from jax.sharding import PartitionSpec as P

EPS = 1e-6
NEG_BIG = -1e30
FLOOR = -0.999e30
LOG2E = math.log2(math.e)
MIB = 1 << 20
VMEM_MIB = 52
F32 = jnp.float32
BF16 = jnp.bfloat16
LANES = 128
SUB = 8
BLOCK = 256
GROUP = 4
SPLITS = 2
PIECES = 16
HID = 4
FAR, RIGHT, OWN, LEFT = range(4)
SLOTS = 6
ROUTES = 4
N_INPUTS, N_OUTS, N_PROJECT = 8, 3, 12
STAT = SUB


def remote(src, dst, ssem, rsem, dev):
    return pltpu.make_async_remote_copy(src_ref=src, dst_ref=dst, send_sem=ssem, recv_sem=rsem,
                                        device_id=dev, device_id_type=pl.DeviceIdType.MESH)


def meet(peers):
    barrier = pltpu.get_barrier_semaphore()
    for dev in peers:
        pl.semaphore_signal(barrier, inc=1, device_id=dev, device_id_type=pl.DeviceIdType.MESH)
    return barrier


def iota(shape, dim):
    return lax.broadcasted_iota(jnp.int32, shape, dim)


def project(seq_block, kv, enter, len_hbm, hid_hbm, gain_hbm, wq_hbm, wk_hbm, wv_hbm, kc_hbm, vc_hbm,
            kbuf, vbuf, kvq, len_ref, hbuf, gain_raw, gain_ref, nbuf, wbuf,
            sem_l, sem_g, sem_h, sem_w, sem_k, sem_v, sem_s, sem_r):
    batch, d_model = hid_hbm.shape
    n_w = wbuf.shape[0]
    spi, y = lax.axis_index('sp'), lax.axis_index('tp')
    c = spi % 2
    partner = {'tp': y, 'sp': spi + 1 - 2 * c}
    base = spi * seq_block
    rows_h = batch // HID
    seq_rows = seq_block * kv
    per_piece = batch // PIECES
    crow = per_piece * seq_rows

    hid_copies = [pltpu.make_async_copy(hid_hbm.at[pl.ds(i * rows_h, rows_h)], hbuf.at[pl.ds(i * rows_h, rows_h)], sem_h.at[i])
                  for i in range(HID)]
    len_copy = pltpu.make_async_copy(len_hbm, len_ref, sem_l)
    gain_copy = pltpu.make_async_copy(gain_hbm, gain_raw, sem_g)

    def w_copy(j, src, first):
        return pltpu.make_async_copy(src.at[:, pl.ds(first, BLOCK)], wbuf.at[j], sem_w.at[j])

    def q_copy(j):
        return w_copy(j, wq_hbm, pl.multiple_of(c * (n_w - 1) * BLOCK + (j - 1) * BLOCK, BLOCK))

    def cache_copies(p):
        part = pl.ds(pl.multiple_of(p * crow, crow), crow)
        return [pltpu.make_async_copy(src.at[part], buf.at[part], sem.at[p])
                for src, buf, sem in ((kc_hbm, kbuf, sem_k), (vc_hbm, vbuf, sem_v))]

    def trade(j):
        slot = kvq.at[c * n_w + j]
        return remote(slot, slot, sem_s.at[j], sem_r.at[j], partner)

    def arrival(j):
        slot = kvq.at[(1 - c) * n_w + j]
        return remote(slot, slot, sem_s.at[j], sem_r.at[j], partner)

    for cp in hid_copies + [gain_copy]:
        cp.start()

    @pl.when(c == 0)
    def _():
        w_copy(0, wk_hbm, 0).start()

    @pl.when(c == 1)
    def _():
        w_copy(0, wv_hbm, 0).start()

    q_copy(1).start()
    len_copy.start()

    step = 2 * SUB
    wide = SUB * LANES

    def norm_rows(r, carry):
        row = pl.ds(pl.multiple_of(r * step, step), step)
        cuts = [slice(w, w + wide) for w in range(0, d_model, wide)]
        total = jnp.zeros((step, 1), F32)
        for cut in cuts:
            v = hbuf[row, cut].astype(F32)
            total = total + jnp.sum(v * v, axis=1, keepdims=True)
        inv = lax.rsqrt(total / d_model + EPS)
        for cut in cuts:
            nbuf[row, cut] = (hbuf[row, cut].astype(F32) * inv * gain_ref[:, cut]).astype(BF16)
        return carry

    gain_copy.wait()
    gain_ref[...] = gain_raw[...].astype(F32).reshape(gain_ref.shape)
    for i in range(HID):
        hid_copies[i].wait()
        if i % 2:
            q_copy(2 + i // 2).start()
        lax.fori_loop(i * rows_h // step, (i + 1) * rows_h // step, norm_rows, 0)
    enter()

    per_step = PIECES // n_w

    def columns(j, carry):
        w_copy(j, wk_hbm, 0).wait()
        for i in range(per_step):
            for cp in cache_copies(j * per_step + i):
                cp.start()

        @pl.when(j > 0)
        def _():
            trade(j - 1).start()

        res = jnp.dot(nbuf[...], wbuf[j], preferred_element_type=F32)
        for i in range(BLOCK // LANES):
            kvq[c * n_w + j, pl.ds(i, batch, stride=BLOCK // LANES), :] = res[:, i * LANES:(i + 1) * LANES]
        return carry

    lax.fori_loop(0, n_w, columns, 0)
    trade(n_w - 1).start()
    len_copy.wait()
    arrival(0).wait_recv()

    pair_row = iota((step, LANES), 0) % kv
    slot_pos = iota((seq_rows, LANES), 0) // kv

    def update(p, carry):
        for cp in cache_copies(p):
            cp.wait()
        for i in range(per_piece):
            b = p * per_piece + i
            here = slot_pos == len_ref[b] - base
            rows = pl.ds(pl.multiple_of(b * seq_rows, step), seq_rows)
            for core, buf in enumerate((kbuf, vbuf)):
                new = kvq[core * n_w, pl.ds(b * kv, 1), :]
                for n in range(1, kv):
                    new = jnp.where(pair_row == n, kvq[core * n_w, pl.ds(b * kv + n, 1), :], new)
                new = jnp.concatenate([new.astype(BF16)] * (seq_rows // step), axis=0)
                buf[rows, :] = jnp.where(here, new, buf[rows, :])
        return carry

    lax.fori_loop(0, PIECES, update, 0)
    for j in range(1, n_w):
        arrival(j).wait_recv()
    for j in range(n_w):
        trade(j).wait_send()


def decode_kernel(seq_block, kv, heads, *refs):
    inputs, wo_hbm, outs = refs[:N_INPUTS], refs[N_INPUTS], refs[N_INPUTS + 1:N_INPUTS + N_OUTS + 1]
    kvq, len_ref, hbuf, *rest = refs[N_INPUTS + N_OUTS + 1:]
    kbuf, vbuf, out_ref = outs

    def first(enter):
        project(seq_block, kv, enter, *inputs, kbuf, vbuf, kvq, len_ref, hbuf, *rest[:N_PROJECT])

    exchange(seq_block, kv, heads, first, kbuf, vbuf, kvq, len_ref, hbuf, wo_hbm, out_ref, *rest[N_PROJECT:])


def exchange(seq_block, kv, heads, first_part, kbuf, vbuf, kvq, len_ref, hbuf, wo_hbm, out_ref,
             acc, pbuf, xsend, xrecv, obuf, lhs, wbuf, ysend, yrecv, gbuf,
             sem_w, sem_ps, sem_pr, sem_xs, sem_xr, sem_os, sem_or, sem_ys, sem_yr,
             sem_fs, sem_fr, sem_ss, sem_sr, sem_ds, sem_dr):
    batch, d_model = out_ref.shape
    spi, y = lax.axis_index('sp'), lax.axis_index('tp')
    sp, ny = lax.axis_size('sp'), lax.axis_size('tp')
    nx = sp // 2
    x, c = spi // 2, spi % 2
    base = spi * seq_block
    seq_rows = seq_block * kv
    n_w = kvq.shape[0] // 2
    unit = batch // (sp * SPLITS * 2)
    ur = unit * heads
    rows = batch // nx
    part = rows // (2 * SPLITS)
    half_d = d_model // 2
    cols = half_d // ny
    hc = cols // 2

    def at_x(d):
        return (x + d + nx) % nx

    def at_y(d):
        return (y + d + ny) % ny

    partner = {'tp': y, 'sp': spi + 1 - 2 * c}
    x_dev = {d: {'tp': y, 'sp': at_x(d) * 2 + c} for d in (1, -1)}
    y_dev = {d: {'tp': at_y(d), 'sp': spi} for d in (1, -1)}

    barrier = meet([partner, *x_dev.values(), *y_dev.values()])
    w_copies = []
    for k in range(ROUTES):
        first = pl.multiple_of(c * half_d + at_y(2 - k) * cols, LANES)
        w_copies.append(pltpu.make_async_copy(wo_hbm.at[:, pl.ds(first, cols)], wbuf.at[k], sem_w.at[k]))
    first_part(lambda: pl.semaphore_wait(barrier, 1 + len(x_dev) + len(y_dev)))
    for cp in w_copies:
        cp.start()

    per = BLOCK // LANES
    tile = GROUP * per
    n_tiles = heads // per
    qrows = GROUP * heads
    krows = GROUP * seq_rows
    row_id, col_id = iota((qrows, krows), 0), iota((qrows, krows), 1)
    same = (row_id % tile // per == col_id // seq_rows) & (row_id // (qrows // kv) == col_id % kv)
    col_row = iota((1, krows), 1)
    col_seq = col_row // seq_rows
    col_pos = col_row % seq_rows // kv
    diag = iota((ur, LANES), 0) == iota((ur, LANES), 1)
    fold = LANES ** -0.5 * LOG2E
    halves = [(core, h) for core in range(2) for h in range(2)]
    groups = [(core, h, g) for core, h in halves for g in range(unit // GROUP)]

    def pair(k, n):
        return remote(acc.at[n, k, 1 - c], pbuf.at[n, k], sem_ps.at[n * ROUTES + k], sem_pr.at[n * ROUTES + k], partner)

    def attend(n):
        def one(k, carry):
            dest = at_x(2 - k)

            def first(core, h, g):
                return (((dest * 2 + core) * SPLITS + n) * 2 + h) * unit + g * GROUP

            scores = []
            for where in groups:
                b0 = first(*where)
                rows8 = pl.ds(pl.multiple_of(b0 * per, tile), tile)
                q = jnp.concatenate([kvq[core * n_w + j, rows8, :] for core in range(2) for j in range(1, n_w)], axis=0)
                keys = kbuf[pl.ds(pl.multiple_of(b0 * seq_rows, krows), krows), :]
                s = lax.dot_general(q.astype(BF16), keys, (((1,), (1,)), ((), ())), preferred_element_type=F32)
                last = jnp.full((1, krows), len_ref[b0] - base, jnp.int32)
                for i in range(1, GROUP):
                    last = jnp.where(col_seq == i, len_ref[b0 + i] - base, last)
                scores.append(jnp.where(same & (col_pos <= last), s * fold, NEG_BIG))
            peaks = [jnp.maximum(jnp.max(s, axis=1, keepdims=True), FLOOR) for s in scores]
            exps = [jnp.exp2(s - m) for s, m in zip(scores, peaks)]
            sums = [jnp.sum(e, axis=1, keepdims=True) for e in exps]
            for where, e in zip(groups, exps):
                core, h, g = where
                values = vbuf[pl.ds(pl.multiple_of(first(*where) * seq_rows, krows), krows), :]
                o = jnp.dot(e.astype(BF16), values, preferred_element_type=F32)
                for t in range(n_tiles):
                    at = (t * (unit // GROUP) + g) * tile
                    acc[n, k, core, h, at:at + tile, :] = o[t * tile:(t + 1) * tile]
            for core, h in halves:
                packed = []
                for stat in (peaks, sums):
                    mine = [s for where, s in zip(groups, stat) if where[:2] == (core, h)]
                    col = jnp.concatenate([s[t * tile:(t + 1) * tile] for t in range(n_tiles) for s in mine], axis=0)
                    spread = jnp.where(diag, jnp.broadcast_to(col, diag.shape), 0.0)
                    packed.append(jnp.sum(spread, axis=0, keepdims=True))
                packed.append(jnp.zeros((STAT - len(packed), LANES), F32))
                acc[n, k, core, h, ur:ur + STAT, :] = jnp.concatenate(packed, axis=0)

            pair(k, n).start()
            return carry

        lax.fori_loop(0, ROUTES, one, 0)

    def column(stat):
        return jnp.sum(jnp.where(diag, jnp.broadcast_to(stat, diag.shape), 0.0), axis=1, keepdims=True)

    def merge(refs):
        both = [(r[ur:ur + 1, :], r[ur + 1:ur + 2, :]) for r in refs]
        peak = functools.reduce(jnp.maximum, [m for m, _ in both])
        scale = [jnp.exp2(m - peak) for m, _ in both]
        denom = sum(l * s for (_, l), s in zip(both, scale))
        total = sum(r[:ur, :] * column(s) for r, s in zip(refs, scale))
        return total, peak, denom

    def merge_into(dst, refs):
        total, peak, denom = merge(refs)
        dst[:ur, :] = total
        dst[ur:ur + STAT, :] = jnp.concatenate([peak, denom, jnp.zeros((STAT - 2, LANES), F32)], axis=0)

    FAR0, FAR1, RAW_R, RAW_L, SUM_R, SUM_L = range(SLOTS)
    ends = ((RAW_L, SUM_R), (RAW_R, SUM_L))

    def ring_copies(send, recv, ssem, rsem, devs):
        return [[remote(send.at[n, i], recv.at[n, i], ssem.at[n * SLOTS + i], rsem.at[n * SLOTS + i],
                        devs[1 if i in (FAR0, RAW_R, SUM_R) else -1]) for i in range(SLOTS)] for n in range(SPLITS)]

    xc = ring_copies(xsend, xrecv, sem_xs, sem_xr, x_dev)
    yc = ring_copies(ysend, yrecv, sem_ys, sem_yr, y_dev)
    oc = [remote(obuf.at[n, c], obuf.at[n, c], sem_os.at[n], sem_or.at[n], partner) for n in range(SPLITS)]

    def both(n, k, h):
        return [acc.at[n, k, c, h], pbuf.at[n, k, h]]

    def x_start(n):
        for k, todo in ((FAR, ((FAR0, 0), (FAR1, 1))), (RIGHT, ((RAW_R, 1),)), (LEFT, ((RAW_L, 0),))):
            pair(k, n).wait_recv()
            for slot, h in todo:
                merge_into(xsend.at[n, slot], both(n, k, h))
                xc[n][slot].start()

    def x_pass(n):
        for came, slot, k, h in ((FAR0, SUM_R, RIGHT, 0), (FAR1, SUM_L, LEFT, 1)):
            xc[n][came].wait_recv()
            merge_into(xsend.at[n, slot], both(n, k, h) + [xrecv.at[n, came]])
            xc[n][slot].start()

    def x_end(n):
        pair(OWN, n).wait_recv()
        for h, came in enumerate(ends):
            for slot in came:
                xc[n][slot].wait_recv()
            total, _, denom = merge(both(n, OWN, h) + [xrecv.at[n, slot] for slot in came])
            obuf[n, c, h * ur:(h + 1) * ur, :] = (total / column(denom)).astype(BF16).astype(F32)
        oc[n].start()

    def y_start(n):
        oc[n].wait_recv()
        for core, h in halves:
            at = core * part + h * unit
            for t in range(n_tiles):
                for i in range(per):
                    head = (t * per + i) * LANES
                    lhs[n, at:at + unit, head:head + LANES] = obuf[
                        n, core, pl.ds(h * ur + t * unit * per + i, unit, stride=per), :]
        for k, first, second in ((FAR, FAR0, FAR1), (RIGHT, SUM_R, RAW_R), (LEFT, RAW_L, SUM_L)):
            if n == 0:
                w_copies[k].wait()
            prod = product(n, k)
            ysend[n, first] = prod[:, :hc]
            ysend[n, second] = prod[:, hc:]
            for slot in (first, second):
                if slot not in (SUM_R, SUM_L):
                    yc[n][slot].start()

    def product(n, k):
        return jnp.dot(lhs[n].astype(BF16), wbuf[k], preferred_element_type=F32)

    def y_pass(n):
        for came, slot in ((FAR0, SUM_R), (FAR1, SUM_L)):
            yc[n][came].wait_recv()
            ysend[n, slot] = ysend[n, slot] + yrecv[n, came]
            yc[n][slot].start()

    f = x + c * (y - x)
    s = y + c * (x - y)
    sent = []

    def go(copy):
        copy.start()
        sent.append(copy)

    def f_dev(d):
        return {'tp': (y + c * d + ny) % ny, 'sp': ((x + (1 - c) * d + nx) % nx) * 2 + c}

    def s_dev(d):
        return {'tp': (y + (1 - c) * d + ny) % ny, 'sp': ((x + c * d + nx) % nx) * 2 + c}

    def block(n, fd, sd):
        return gbuf.at[n, c, (f + fd + nx) % nx, (s + sd + ny) % ny]

    def kind(d, is_half):
        return is_half * 2 + (d > 0)

    def along(ring, n, fd, sd, d, is_half=False):
        ref = block(n, fd, sd)
        if is_half:
            ref = ref.at[0 if d > 0 else 1]
        if ring == 'f':
            i = n * ROUTES + kind(d, is_half)
            return remote(ref, ref, sem_fs.at[i], sem_fr.at[i], f_dev(d))
        i = (n * nx + fd % nx) * ROUTES + kind(d, is_half)
        return remote(ref, ref, sem_ss.at[i], sem_sr.at[i], s_dev(d))

    def over(n, fd, sd):
        i = (n * nx + fd % nx) * ny + sd % ny
        ref = block(n, fd, sd)
        return remote(ref, ref, sem_ds.at[i], sem_dr.at[i], partner)

    def place(n, ci, fi, si, swap):
        xi, yi = fi + swap * (si - fi), si + swap * (fi - si)
        for h in range(2):
            at = pl.ds(pl.multiple_of(ci * half_d + yi * cols + h * hc, LANES), hc)
            for core in range(2):
                first = pl.multiple_of(xi * rows + (core * SPLITS + n) * part, part)
                out_ref[pl.ds(first, part), at] = gbuf[n, ci, fi, si, h, core * part:(core + 1) * part, :].astype(BF16)

    def place_here(n, fd, sd):
        place(n, c, (f + fd + nx) % nx, (s + sd + ny) % ny, c)

    def spread(n, fd):
        for d in (1, -1):
            go(along('s', n, fd, 0, d))
        go(over(n, fd, 0))

    def y_end(n):
        if n == 0:
            w_copies[OWN].wait()
        own = product(n, OWN)
        for h, came in enumerate(ends):
            for slot in came:
                yc[n][slot].wait_recv()
            total = own[:, h * hc:(h + 1) * hc] + yrecv[n, came[0]] + yrecv[n, came[1]]
            at = pl.ds(pl.multiple_of(c * half_d + y * cols + h * hc, LANES), hc)
            kept = jnp.concatenate([hbuf[pl.ds(pl.multiple_of(x * rows + (core * SPLITS + n) * part, part), part), at]
                                    for core in range(2)], axis=0)
            gbuf[n, c, f, s, h] = (kept.astype(F32) + total).astype(BF16).astype(F32)
        for d in (1, -1):
            go(along('f', n, 0, 0, d))
        spread(n, 0)
        place_here(n, 0, 0)

    def pass_on(ring, n, fd, sd, d):
        along(ring, n, fd, sd, d).wait_recv()
        go(along(ring, n, fd, sd, d, True))

    def f_ring(n):
        for d in (1, -1):
            pass_on('f', n, -d, 0, d)
            spread(n, -d)
        for d in (1, -1):
            place_here(n, -d, 0)

    def f_end(n):
        for d in (1, -1):
            along('f', n, 2, 0, d, True).wait_recv()
        spread(n, 2)
        place_here(n, 2, 0)

    def s_ring(n, fd):
        for d in (1, -1):
            pass_on('s', n, fd, -d, d)
            go(over(n, fd, -d))
        for d in (1, -1):
            place_here(n, fd, -d)

    def s_end(n, fd):
        for d in (1, -1):
            along('s', n, fd, 2, d, True).wait_recv()
        go(over(n, fd, 2))
        place_here(n, fd, 2)

    def take(n, fd, sd):
        i = (n * nx + fd % nx) * ny + sd % ny
        fi, si = (s + fd + nx) % nx, (f + sd + ny) % ny
        ref = gbuf.at[n, 1 - c, fi, si]
        remote(ref, ref, sem_ds.at[i], sem_dr.at[i], partner).wait_recv()
        place(n, 1 - c, fi, si, 1 - c)

    def stage(n, i):
        if i == 0:
            f_ring(n)
            s_ring(n, 0)
        elif i == 1:
            f_end(n)
            s_ring(n, -1)
            s_ring(n, 1)
            s_end(n, 0)
        elif i == 2:
            for fd in (0, -1, 1):
                take(n, fd, 0)
            s_ring(n, 2)
            s_end(n, -1)
            s_end(n, 1)
        else:
            for fd, sd in ((2, 0), (0, -1), (0, 1), (0, 2), (-1, -1), (-1, 1), (1, -1), (1, 1)):
                take(n, fd, sd)
            s_end(n, 2)

    attend(0)
    x_start(0)
    attend(1)
    x_pass(0)
    x_start(1)
    x_end(0)
    x_pass(1)
    y_start(0)
    x_end(1)
    y_pass(0)
    y_start(1)
    y_end(0)
    y_pass(1)
    y_end(1)
    for i in range(ROUTES):
        for n in range(SPLITS):
            stage(n, i)
    for n in range(SPLITS):
        for fd, sd in ((2, -1), (2, 1), (-1, 2), (1, 2), (2, 2)):
            take(n, fd, sd)
    for n in range(SPLITS):
        for k in range(ROUTES):
            pair(k, n).wait_send()
    for cp in xc + yc:
        for one in cp:
            one.wait_send()
    for cp in oc + sent:
        cp.wait_send()


def solution(mesh):
    cache_spec = P('dp', 'sp', 'tp', None)
    sp = mesh.shape['sp']
    tp = mesh.shape['tp']

    def local_step(hidden, lengths, k_cache, v_cache, norm_gain, w_query, w_key, w_value, w_out):
        batch, seq_block, kv, head_dim = k_cache.shape
        d_model = hidden.shape[1]
        width = w_query.shape[1]
        heads = width // head_dim
        n_w = width // (2 * BLOCK) + 1
        flat = batch * seq_block * kv
        hbm = pl.BlockSpec(memory_space=pltpu.HBM)
        vmem = pl.BlockSpec(memory_space=pltpu.VMEM)
        shape = jax.ShapeDtypeStruct
        buf = pltpu.VMEM

        def dma(*shapes):
            return [pltpu.SemaphoreType.DMA(s) if s else pltpu.SemaphoreType.DMA for s in shapes]

        nx = sp // 2
        rows = batch // nx
        cols = d_model // (2 * tp)
        ur = batch // (sp * SPLITS * 2) * heads
        travel = buf((SPLITS, SLOTS, ur + STAT, head_dim), F32)
        yblock = buf((SPLITS, SLOTS, rows // SPLITS, cols // 2), F32)
        n_x, n_f = SPLITS * SLOTS, SPLITS * ROUTES
        n_s = n_f * nx
        n_d = SPLITS * nx * tp
        k_new, v_new, out = pl.pallas_call(
            functools.partial(decode_kernel, seq_block, kv, heads),
            out_shape=(buf((flat, head_dim), BF16), buf((flat, head_dim), BF16), buf((batch, d_model), BF16)),
            in_specs=[hbm] * (N_INPUTS + 1),
            out_specs=(vmem, vmem, vmem),
            scratch_shapes=[
                buf((2 * n_w, batch * BLOCK // head_dim, head_dim), F32),
                pltpu.SMEM((batch,), jnp.int32),
                buf((batch, d_model), BF16),
                buf((d_model,), BF16),
                buf((1, d_model), F32),
                buf((batch, d_model), BF16),
                buf((n_w, d_model, BLOCK), BF16),
                *dma((), (), (HID,), (n_w,), (PIECES,), (PIECES,), (n_w,), (n_w,)),
                buf((SPLITS, ROUTES, 2, 2, ur + STAT, head_dim), F32),
                buf((SPLITS, ROUTES, 2, ur + STAT, head_dim), F32),
                travel, travel,
                buf((SPLITS, 2, 2 * ur, head_dim), F32),
                buf((SPLITS, rows // SPLITS, width), F32),
                buf((ROUTES, width, cols), BF16),
                yblock, yblock,
                buf((SPLITS, 2, nx, tp, 2, rows // SPLITS, cols // 2), F32),
                *dma((ROUTES,), (n_f,), (n_f,), (n_x,), (n_x,), (SPLITS,), (SPLITS,), (n_x,), (n_x,),
                     (n_f,), (n_f,), (n_s,), (n_s,), (n_d,), (n_d,)),
            ],
            compiler_params=pltpu.CompilerParams(collective_id=0, has_side_effects=True, vmem_limit_bytes=VMEM_MIB * MIB),
            name='decode_step',
        )(lengths, hidden, norm_gain, w_query, w_key, w_value,
          k_cache.reshape(flat, head_dim), v_cache.reshape(flat, head_dim), w_out)
        return out, k_new.reshape(k_cache.shape), v_new.reshape(v_cache.shape)

    return jax.shard_map(
        local_step,
        mesh=mesh,
        in_specs=(P('dp', None), P('dp'), cache_spec, cache_spec, P(None), P(None, 'tp'), P(None, 'tp'), P(None, 'tp'), P('tp', None)),
        out_specs=(P('dp', None), cache_spec, cache_spec),
        check_vma=False,
    )
```

time: 296 us -> 71.7 us (0.24)
  waiting for transfers between devices: 158 us -> 0 us
  Pallas kernels: 0 us -> 65.3 us
  blocking collectives: 54.9 us -> 0 us
  matrix products: 36.9 us -> 0 us
  other arithmetic: 26.8 us -> 0 us
  between operations: 14.3 us -> 0.64 us
    psum x2 -> x0, waiting for transfers between devices: 158 us -> none  [the longest x1 123 us: local_step(): head_sum = lax.psum(part_out, 'tp')]
    pallas_call x0 -> x1, Pallas kernels: none -> 65.3 us  [local_step(): pl.pallas_call(functools.partial(decode_kernel, seq_block, kv, heads), ou...]
    dot_general x6 -> x0, matrix products: 36.9 us -> none  [the longest x1 13.5 us: local_step(): part_out = jnp.dot(attn_out, w_out, preferred_element_type=jnp.float32)]
    psum x1 -> x0, blocking collectives: 28 us -> none  [local_step(): lax.psum((local_acc * rescale, local_denom * rescale), 'sp')]
    pmax x1 -> x0, blocking collectives: 26.9 us -> none  [local_step(): global_peak = lax.pmax(local_peak, 'sp')]
    select_n x1 -> x0, other arithmetic: 13.8 us -> none  [local_step(): jnp.where(at_slot, new_key.reshape(batch, 1, kv_local, head_dim), k_cache)]
    convert_element_type x3 -> x0, other arithmetic: 8.3 us -> none  [the longest x1 6.35 us: local_step(): hidden_out = (hid_f32 + head_sum).astype(jnp.bfloat16)]
    unnamed x16 -> x3, local copies, waits for them, and re-layouts: 0.97 us -> 5.69 us
  transfers between devices with their start and end apart: 2 -> 0, of which waited for: 2 -> 0; matrix products, arithmetic and copies ran while one was open for 0% -> 0% of each run, Pallas kernels for 0% -> 0%
where the time goes in v2:
time: 71.7 us
  Pallas kernels  65.3 us (91%)
  local copies, waits for them, and re-layouts  5.69 us (8%)
    pallas_call x1, Pallas kernels, local_step(): pl.pallas_call(functools.partial(decode_kernel, seq_block, kv, heads), ou...  65.3 us
    unnamed x3, local copies, waits for them, and re-layouts  5.69 us

profile of v2, /device:TPU:97, one launch (start us, length us, event | category | flops | bytes accessed | tf_op | source)
XLA Modules:
  0.0 71.7 jit_solution(13355273246242966082)
XLA Ops:
  0.6 65.3 %decode_step.1 = (bf16[16384,128]{1,0:T(8,128)(2,1)S(1)}, bf16[16384,128]{1,0:T(8,128)(2,1)S(1)}, bf16[256,6144]{1,0:T(8,128)(2,1)S(1)}) custom-call(s32[256]{0:T(256)} %refs_0_.1, bf16[256,6144]{1,0:T(8,128)(2,1)} %refs_1_.1, bf16[6144]{0:T(1024)(128)(2,1)} %refs_2_.1, bf16[6144,1536]{1,0:T(8,128)(2,1)} %refs_3_.1, bf16[6144,256]{1,0:T(8,128)(2,1)} %refs_4_.1, ...), custom_call_target="tpu_custom_call" | custom-call | tf_op jit(solution)/shard_map/decode_step/pallas_call | solution.py:547
  66.0 1.7 %copy.15 = bf16[256,6144]{1,0:T(8,128)(2,1)} copy(bf16[256,6144]{1,0:T(8,128)(2,1)S(1)} %get-tuple-element.9) | data formatting | bytes 6291456
  67.6 2.0 %copy.16 = bf16[256,32,2,128]{3,2,1,0:T(2,128)(2,1)} copy(bf16[256,32,2,128]{3,2,1,0:T(2,128)(2,1)S(1)} %bitcast.5) | data formatting | bytes 8388608
  69.7 2.0 %copy.17 = bf16[256,32,2,128]{3,2,1,0:T(2,128)(2,1)} copy(bf16[256,32,2,128]{3,2,1,0:T(2,128)(2,1)S(1)} %bitcast.4) | data formatting | bytes 8388608

commit v3 on v2

--- a/solution.py
+++ b/solution.py
@@ -24,7 +24,7 @@
 PIECES = 16
 HID = 4
 FAR, RIGHT, OWN, LEFT = range(4)
-SLOTS = 6
+AWAY = 3
 ROUTES = 4
 N_INPUTS, N_OUTS, N_PROJECT = 8, 3, 12
 STAT = SUB
@@ -84,8 +84,11 @@
         slot = kvq.at[(1 - c) * n_w + j]
         return remote(slot, slot, sem_s.at[j], sem_r.at[j], partner)
 
-    for cp in hid_copies + [gain_copy]:
+    for cp in hid_copies + [gain_copy, len_copy]:
         cp.start()
+    gain_copy.wait()
+    gain_ref[...] = gain_raw[...].astype(F32).reshape(gain_ref.shape)
+    hid_copies[0].wait()
 
     @pl.when(c == 0)
     def _():
@@ -94,9 +97,6 @@
     @pl.when(c == 1)
     def _():
         w_copy(0, wv_hbm, 0).start()
-
-    q_copy(1).start()
-    len_copy.start()
 
     step = 2 * SUB
     wide = SUB * LANES
@@ -113,12 +113,10 @@
             nbuf[row, cut] = (hbuf[row, cut].astype(F32) * inv * gain_ref[:, cut]).astype(BF16)
         return carry
 
-    gain_copy.wait()
-    gain_ref[...] = gain_raw[...].astype(F32).reshape(gain_ref.shape)
     for i in range(HID):
-        hid_copies[i].wait()
-        if i % 2:
-            q_copy(2 + i // 2).start()
+        if i:
+            hid_copies[i].wait()
+            q_copy(i).start()
         lax.fori_loop(i * rows_h // step, (i + 1) * rows_h // step, norm_rows, 0)
     enter()
 
@@ -167,6 +165,14 @@
         arrival(j).wait_recv()
     for j in range(n_w):
         trade(j).wait_send()
+
+
+def store_kernel(*refs):
+    copies = [pltpu.make_async_copy(refs[i], refs[N_OUTS + i], refs[-1].at[i]) for i in range(N_OUTS)]
+    for cp in copies:
+        cp.start()
+    for cp in copies:
+        cp.wait()
 
 
 def decode_kernel(seq_block, kv, heads, *refs):
@@ -207,8 +213,8 @@
         return (y + d + ny) % ny
 
     partner = {'tp': y, 'sp': spi + 1 - 2 * c}
-    x_dev = {d: {'tp': y, 'sp': at_x(d) * 2 + c} for d in (1, -1)}
-    y_dev = {d: {'tp': at_y(d), 'sp': spi} for d in (1, -1)}
+    x_dev = {d: {'tp': y, 'sp': at_x(d) * 2 + c} for d in (2, 1, -1)}
+    y_dev = {d: {'tp': at_y(d), 'sp': spi} for d in (2, 1, -1)}
 
     barrier = meet([partner, *x_dev.values(), *y_dev.values()])
     w_copies = []
@@ -296,41 +302,38 @@
         dst[:ur, :] = total
         dst[ur:ur + STAT, :] = jnp.concatenate([peak, denom, jnp.zeros((STAT - 2, LANES), F32)], axis=0)
 
-    FAR0, FAR1, RAW_R, RAW_L, SUM_R, SUM_L = range(SLOTS)
-    ends = ((RAW_L, SUM_R), (RAW_R, SUM_L))
-
-    def ring_copies(send, recv, ssem, rsem, devs):
-        return [[remote(send.at[n, i], recv.at[n, i], ssem.at[n * SLOTS + i], rsem.at[n * SLOTS + i],
-                        devs[1 if i in (FAR0, RAW_R, SUM_R) else -1]) for i in range(SLOTS)] for n in range(SPLITS)]
-
-    xc = ring_copies(xsend, xrecv, sem_xs, sem_xr, x_dev)
-    yc = ring_copies(ysend, yrecv, sem_ys, sem_yr, y_dev)
+    def sends(send, recv, ssem, rsem, devs):
+        return [[remote(send.at[n, i], recv.at[n, i], ssem.at[n * AWAY + i], rsem.at[n * AWAY + i], devs[d])
+                 for i, d in enumerate((2, 1, -1))] for n in range(SPLITS)]
+
+    xc = sends(xsend, xrecv, sem_xs, sem_xr, x_dev)
+    yc = sends(ysend, yrecv, sem_ys, sem_yr, y_dev)
     oc = [remote(obuf.at[n, c], obuf.at[n, c], sem_os.at[n], sem_or.at[n], partner) for n in range(SPLITS)]
+    away = (FAR, RIGHT, LEFT)
 
     def both(n, k, h):
         return [acc.at[n, k, c, h], pbuf.at[n, k, h]]
 
     def x_start(n):
-        for k, todo in ((FAR, ((FAR0, 0), (FAR1, 1))), (RIGHT, ((RAW_R, 1),)), (LEFT, ((RAW_L, 0),))):
+        for i, k in enumerate(away):
             pair(k, n).wait_recv()
-            for slot, h in todo:
-                merge_into(xsend.at[n, slot], both(n, k, h))
-                xc[n][slot].start()
-
-    def x_pass(n):
-        for came, slot, k, h in ((FAR0, SUM_R, RIGHT, 0), (FAR1, SUM_L, LEFT, 1)):
-            xc[n][came].wait_recv()
-            merge_into(xsend.at[n, slot], both(n, k, h) + [xrecv.at[n, came]])
-            xc[n][slot].start()
+            for h in range(2):
+                merge_into(xsend.at[n, i, h], both(n, k, h))
+            xc[n][i].start()
 
     def x_end(n):
         pair(OWN, n).wait_recv()
-        for h, came in enumerate(ends):
-            for slot in came:
-                xc[n][slot].wait_recv()
-            total, _, denom = merge(both(n, OWN, h) + [xrecv.at[n, slot] for slot in came])
+        for cp in xc[n]:
+            cp.wait_recv()
+        for h in range(2):
+            total, _, denom = merge(both(n, OWN, h) + [xrecv.at[n, i, h] for i in range(AWAY)])
             obuf[n, c, h * ur:(h + 1) * ur, :] = (total / column(denom)).astype(BF16).astype(F32)
         oc[n].start()
+
+    def product(n, k):
+        if n == 0:
+            w_copies[k].wait()
+        return jnp.dot(lhs[n].astype(BF16), wbuf[k], preferred_element_type=F32)
 
     def y_start(n):
         oc[n].wait_recv()
@@ -341,24 +344,11 @@
                     head = (t * per + i) * LANES
                     lhs[n, at:at + unit, head:head + LANES] = obuf[
                         n, core, pl.ds(h * ur + t * unit * per + i, unit, stride=per), :]
-        for k, first, second in ((FAR, FAR0, FAR1), (RIGHT, SUM_R, RAW_R), (LEFT, RAW_L, SUM_L)):
-            if n == 0:
-                w_copies[k].wait()
+        for i, k in enumerate(away):
             prod = product(n, k)
-            ysend[n, first] = prod[:, :hc]
-            ysend[n, second] = prod[:, hc:]
-            for slot in (first, second):
-                if slot not in (SUM_R, SUM_L):
-                    yc[n][slot].start()
-
-    def product(n, k):
-        return jnp.dot(lhs[n].astype(BF16), wbuf[k], preferred_element_type=F32)
-
-    def y_pass(n):
-        for came, slot in ((FAR0, SUM_R), (FAR1, SUM_L)):
-            yc[n][came].wait_recv()
-            ysend[n, slot] = ysend[n, slot] + yrecv[n, came]
-            yc[n][slot].start()
+            for h in range(2):
+                ysend[n, i, h] = prod[:, h * hc:(h + 1) * hc]
+            yc[n][i].start()
 
     f = x + c * (y - x)
     s = y + c * (x - y)
@@ -412,13 +402,11 @@
         go(over(n, fd, 0))
 
     def y_end(n):
-        if n == 0:
-            w_copies[OWN].wait()
         own = product(n, OWN)
-        for h, came in enumerate(ends):
-            for slot in came:
-                yc[n][slot].wait_recv()
-            total = own[:, h * hc:(h + 1) * hc] + yrecv[n, came[0]] + yrecv[n, came[1]]
+        for cp in yc[n]:
+            cp.wait_recv()
+        for h in range(2):
+            total = sum([yrecv[n, i, h] for i in range(AWAY)], own[:, h * hc:(h + 1) * hc])
             at = pl.ds(pl.multiple_of(c * half_d + y * cols + h * hc, LANES), hc)
             kept = jnp.concatenate([hbuf[pl.ds(pl.multiple_of(x * rows + (core * SPLITS + n) * part, part), part), at]
                                     for core in range(2)], axis=0)
@@ -488,16 +476,12 @@
     attend(0)
     x_start(0)
     attend(1)
-    x_pass(0)
     x_start(1)
     x_end(0)
-    x_pass(1)
     y_start(0)
     x_end(1)
-    y_pass(0)
     y_start(1)
     y_end(0)
-    y_pass(1)
     y_end(1)
     for i in range(ROUTES):
         for n in range(SPLITS):
@@ -539,9 +523,9 @@
         rows = batch // nx
         cols = d_model // (2 * tp)
         ur = batch // (sp * SPLITS * 2) * heads
-        travel = buf((SPLITS, SLOTS, ur + STAT, head_dim), F32)
-        yblock = buf((SPLITS, SLOTS, rows // SPLITS, cols // 2), F32)
-        n_x, n_f = SPLITS * SLOTS, SPLITS * ROUTES
+        travel = buf((SPLITS, AWAY, 2, ur + STAT, head_dim), F32)
+        yblock = buf((SPLITS, AWAY, 2, rows // SPLITS, cols // 2), F32)
+        n_x, n_f = SPLITS * AWAY, SPLITS * ROUTES
         n_s = n_f * nx
         n_d = SPLITS * nx * tp
         k_new, v_new, out = pl.pallas_call(
@@ -573,6 +557,16 @@
             name='decode_step',
         )(lengths, hidden, norm_gain, w_query, w_key, w_value,
           k_cache.reshape(flat, head_dim), v_cache.reshape(flat, head_dim), w_out)
+        results = (k_new, v_new, out)
+        k_new, v_new, out = pl.pallas_call(
+            store_kernel,
+            out_shape=tuple(shape(r.shape, r.dtype) for r in results),
+            in_specs=[vmem] * N_OUTS,
+            out_specs=(hbm,) * N_OUTS,
+            scratch_shapes=dma((N_OUTS,)),
+            compiler_params=pltpu.CompilerParams(vmem_limit_bytes=MIB),
+            name='store',
+        )(*results)
         return out, k_new.reshape(k_cache.shape), v_new.reshape(v_cache.shape)
 
     return jax.shard_map(

time: 71.7 us -> 66.5 us (0.927)
  local copies, waits for them, and re-layouts: 5.69 us -> 0 us
    unnamed x3 -> x0, local copies, waits for them, and re-layouts: 5.69 us -> none
    pallas_call x0 -> x1, Pallas kernels: none -> 4.33 us  [local_step(): pl.pallas_call(store_kernel, out_shape=tuple((shape(r.shape, r.dtype) for...]
    pallas_call x1, Pallas kernels: 65.3 us -> 61.5 us  [local_step(): pl.pallas_call(functools.partial(decode_kernel, seq_block, kv, heads), ou...]
where the time goes in v3:
time: 66.5 us; the launch traced here: 66.4 us
  Pallas kernels  65.8 us (99%)
    pallas_call x1, Pallas kernels, local_step(): pl.pallas_call(functools.partial(decode_kernel, seq_block, kv, heads), ou...  61.5 us
    pallas_call x1, Pallas kernels, local_step(): pl.pallas_call(store_kernel, out_shape=tuple((shape(r.shape, r.dtype) for...  4.33 us

profile of v3, /device:TPU:97, one launch (start us, length us, event | category | flops | bytes accessed | tf_op | source)
XLA Modules:
  0.0 66.4 jit_solution(6159774224082796427)
XLA Ops:
  0.6 61.5 %decode_step.1 = (bf16[16384,128]{1,0:T(8,128)(2,1)S(1)}, bf16[16384,128]{1,0:T(8,128)(2,1)S(1)}, bf16[256,6144]{1,0:T(8,128)(2,1)S(1)}) custom-call(s32[256]{0:T(256)} %refs_0_.1, bf16[256,6144]{1,0:T(8,128)(2,1)} %refs_1_.1, bf16[6144]{0:T(1024)(128)(2,1)} %refs_2_.1, bf16[6144,1536]{1,0:T(8,128)(2,1)} %refs_3_.1, bf16[6144,256]{1,0:T(8,128)(2,1)} %refs_4_.1, ...), custom_call_target="tpu_custom_call" | custom-call | tf_op jit(solution)/shard_map/decode_step/pallas_call | solution.py:531
  62.1 4.3 %store.1 = (bf16[16384,128]{1,0:T(8,128)(2,1)}, bf16[16384,128]{1,0:T(8,128)(2,1)}, bf16[256,6144]{1,0:T(8,128)(2,1)}) custom-call(bf16[16384,128]{1,0:T(8,128)(2,1)S(1)} %get-tuple-element.9.refs_0_, bf16[16384,128]{1,0:T(8,128)(2,1)S(1)} %get-tuple-element.10.refs_1_, bf16[256,6144]{1,0:T(8,128)(2,1)S(1)} %get-tuple-element.11.refs_2_), custom_call_target="tpu_custom_call" | custom-call | tf_op jit(solution)/shard_map/store/pallas_call | solution.py:561

commit v4 on v3

--- a/solution.py
+++ b/solution.py
@@ -23,7 +23,9 @@
 SPLITS = 2
 PIECES = 16
 HID = 4
-FAR, RIGHT, OWN, LEFT = range(4)
+FAR, RIGHT, LEFT, OWN = range(4)
+HOPS = (2, 1, -1, 0)
+LAG = 3
 AWAY = 3
 ROUTES = 4
 N_INPUTS, N_OUTS, N_PROJECT = 8, 3, 12
@@ -90,13 +92,16 @@
     gain_ref[...] = gain_raw[...].astype(F32).reshape(gain_ref.shape)
     hid_copies[0].wait()
 
-    @pl.when(c == 0)
-    def _():
-        w_copy(0, wk_hbm, 0).start()
-
-    @pl.when(c == 1)
-    def _():
-        w_copy(0, wv_hbm, 0).start()
+    q_copy(1).start()
+
+    def kv_start():
+        @pl.when(c == 0)
+        def _():
+            w_copy(0, wk_hbm, 0).start()
+
+        @pl.when(c == 1)
+        def _():
+            w_copy(0, wv_hbm, 0).start()
 
     step = 2 * SUB
     wide = SUB * LANES
@@ -116,21 +121,25 @@
     for i in range(HID):
         if i:
             hid_copies[i].wait()
-            q_copy(i).start()
+            if i + 1 < n_w:
+                q_copy(i + 1).start()
+            else:
+                kv_start()
         lax.fori_loop(i * rows_h // step, (i + 1) * rows_h // step, norm_rows, 0)
     enter()
 
     per_step = PIECES // n_w
 
-    def columns(j, carry):
+    def columns(it, carry):
+        j = (it + 1) % n_w
         w_copy(j, wk_hbm, 0).wait()
         for i in range(per_step):
-            for cp in cache_copies(j * per_step + i):
+            for cp in cache_copies(it * per_step + i):
                 cp.start()
 
-        @pl.when(j > 0)
+        @pl.when(it > 0)
         def _():
-            trade(j - 1).start()
+            trade(it).start()
 
         res = jnp.dot(nbuf[...], wbuf[j], preferred_element_type=F32)
         for i in range(BLOCK // LANES):
@@ -138,16 +147,18 @@
         return carry
 
     lax.fori_loop(0, n_w, columns, 0)
-    trade(n_w - 1).start()
+    trade(0).start()
     len_copy.wait()
-    arrival(0).wait_recv()
+    for p in range(PIECES):
+        for cp in cache_copies(p):
+            cp.wait()
+    for j in range(1, n_w):
+        arrival(j).wait_recv()
 
     pair_row = iota((step, LANES), 0) % kv
     slot_pos = iota((seq_rows, LANES), 0) // kv
 
     def update(p, carry):
-        for cp in cache_copies(p):
-            cp.wait()
         for i in range(per_piece):
             b = p * per_piece + i
             here = slot_pos == len_ref[b] - base
@@ -160,11 +171,12 @@
                 buf[rows, :] = jnp.where(here, new, buf[rows, :])
         return carry
 
-    lax.fori_loop(0, PIECES, update, 0)
-    for j in range(1, n_w):
-        arrival(j).wait_recv()
-    for j in range(n_w):
-        trade(j).wait_send()
+    def new_tokens():
+        lax.fori_loop(0, PIECES, update, 0)
+        for j in range(n_w):
+            trade(j).wait_send()
+
+    return arrival(0).wait_recv, new_tokens
 
 
 def store_kernel(*refs):
@@ -181,13 +193,13 @@
     kbuf, vbuf, out_ref = outs
 
     def first(enter):
-        project(seq_block, kv, enter, *inputs, kbuf, vbuf, kvq, len_ref, hbuf, *rest[:N_PROJECT])
+        return project(seq_block, kv, enter, *inputs, kbuf, vbuf, kvq, len_ref, hbuf, *rest[:N_PROJECT])
 
     exchange(seq_block, kv, heads, first, kbuf, vbuf, kvq, len_ref, hbuf, wo_hbm, out_ref, *rest[N_PROJECT:])
 
 
 def exchange(seq_block, kv, heads, first_part, kbuf, vbuf, kvq, len_ref, hbuf, wo_hbm, out_ref,
-             acc, pbuf, xsend, xrecv, obuf, lhs, wbuf, ysend, yrecv, gbuf,
+             score_a, score_b, newest, acc, pbuf, xsend, xrecv, obuf, lhs, wbuf, ysend, yrecv, gbuf,
              sem_w, sem_ps, sem_pr, sem_xs, sem_xr, sem_os, sem_or, sem_ys, sem_yr,
              sem_fs, sem_fr, sem_ss, sem_sr, sem_ds, sem_dr):
     batch, d_model = out_ref.shape
@@ -219,9 +231,9 @@
     barrier = meet([partner, *x_dev.values(), *y_dev.values()])
     w_copies = []
     for k in range(ROUTES):
-        first = pl.multiple_of(c * half_d + at_y(2 - k) * cols, LANES)
-        w_copies.append(pltpu.make_async_copy(wo_hbm.at[:, pl.ds(first, cols)], wbuf.at[k], sem_w.at[k]))
-    first_part(lambda: pl.semaphore_wait(barrier, 1 + len(x_dev) + len(y_dev)))
+        col = pl.multiple_of(c * half_d + at_y(HOPS[k]) * cols, LANES)
+        w_copies.append(pltpu.make_async_copy(wo_hbm.at[:, pl.ds(col, cols)], wbuf.at[k], sem_w.at[k]))
+    new_arrived, new_tokens = first_part(lambda: pl.semaphore_wait(barrier, 1 + len(x_dev) + len(y_dev)))
     for cp in w_copies:
         cp.start()
 
@@ -243,48 +255,44 @@
     def pair(k, n):
         return remote(acc.at[n, k, 1 - c], pbuf.at[n, k], sem_ps.at[n * ROUTES + k], sem_pr.at[n * ROUTES + k], partner)
 
-    def attend(n):
-        def one(k, carry):
-            dest = at_x(2 - k)
-
-            def first(core, h, g):
-                return (((dest * 2 + core) * SPLITS + n) * 2 + h) * unit + g * GROUP
-
-            scores = []
-            for where in groups:
-                b0 = first(*where)
-                rows8 = pl.ds(pl.multiple_of(b0 * per, tile), tile)
-                q = jnp.concatenate([kvq[core * n_w + j, rows8, :] for core in range(2) for j in range(1, n_w)], axis=0)
-                keys = kbuf[pl.ds(pl.multiple_of(b0 * seq_rows, krows), krows), :]
-                s = lax.dot_general(q.astype(BF16), keys, (((1,), (1,)), ((), ())), preferred_element_type=F32)
-                last = jnp.full((1, krows), len_ref[b0] - base, jnp.int32)
-                for i in range(1, GROUP):
-                    last = jnp.where(col_seq == i, len_ref[b0 + i] - base, last)
-                scores.append(jnp.where(same & (col_pos <= last), s * fold, NEG_BIG))
-            peaks = [jnp.maximum(jnp.max(s, axis=1, keepdims=True), FLOOR) for s in scores]
-            exps = [jnp.exp2(s - m) for s, m in zip(scores, peaks)]
-            sums = [jnp.sum(e, axis=1, keepdims=True) for e in exps]
-            for where, e in zip(groups, exps):
-                core, h, g = where
-                values = vbuf[pl.ds(pl.multiple_of(first(*where) * seq_rows, krows), krows), :]
-                o = jnp.dot(e.astype(BF16), values, preferred_element_type=F32)
-                for t in range(n_tiles):
-                    at = (t * (unit // GROUP) + g) * tile
-                    acc[n, k, core, h, at:at + tile, :] = o[t * tile:(t + 1) * tile]
-            for core, h in halves:
-                packed = []
-                for stat in (peaks, sums):
-                    mine = [s for where, s in zip(groups, stat) if where[:2] == (core, h)]
-                    col = jnp.concatenate([s[t * tile:(t + 1) * tile] for t in range(n_tiles) for s in mine], axis=0)
-                    spread = jnp.where(diag, jnp.broadcast_to(col, diag.shape), 0.0)
-                    packed.append(jnp.sum(spread, axis=0, keepdims=True))
-                packed.append(jnp.zeros((STAT - len(packed), LANES), F32))
-                acc[n, k, core, h, ur:ur + STAT, :] = jnp.concatenate(packed, axis=0)
-
-            pair(k, n).start()
-            return carry
-
-        lax.fori_loop(0, ROUTES, one, 0)
+    def first(n, k, core, h, g):
+        dest = at_x(HOPS[k])
+        return (((dest * 2 + core) * SPLITS + n) * 2 + h) * unit + g * GROUP
+
+    def score(n, k, sbuf):
+        for at, where in enumerate(groups):
+            b0 = first(n, k, *where)
+            rows8 = pl.ds(pl.multiple_of(b0 * per, tile), tile)
+            q = jnp.concatenate([kvq[core * n_w + j, rows8, :] for core in range(2) for j in range(1, n_w)], axis=0)
+            keys = kbuf[pl.ds(pl.multiple_of(b0 * seq_rows, krows), krows), :]
+            s = lax.dot_general(q.astype(BF16), keys, (((1,), (1,)), ((), ())), preferred_element_type=F32)
+            last = jnp.full((1, krows), len_ref[b0] - base, jnp.int32)
+            for i in range(1, GROUP):
+                last = jnp.where(col_seq == i, len_ref[b0 + i] - base, last)
+            sbuf[at] = jnp.where(same & (col_pos < last), s * fold, NEG_BIG)
+
+    def finish(n, k, sbuf):
+        stats = []
+        for at, where in enumerate(groups):
+            core, h, g = where
+            s = sbuf[at]
+            m = jnp.maximum(jnp.max(s, axis=1, keepdims=True), FLOOR)
+            e = jnp.exp2(s - m)
+            stats.append((m, jnp.sum(e, axis=1, keepdims=True)))
+            values = vbuf[pl.ds(pl.multiple_of(first(n, k, *where) * seq_rows, krows), krows), :]
+            o = jnp.dot(e.astype(BF16), values, preferred_element_type=F32)
+            for t in range(n_tiles):
+                row = (t * (unit // GROUP) + g) * tile
+                acc[n, k, core, h, row:row + tile, :] = o[t * tile:(t + 1) * tile]
+        for core, h in halves:
+            mine = [stat for where, stat in zip(groups, stats) if where[:2] == (core, h)]
+            packed = []
+            for which in range(2):
+                col = jnp.concatenate([stat[which][t * tile:(t + 1) * tile] for t in range(n_tiles) for stat in mine], axis=0)
+                packed.append(jnp.sum(jnp.where(diag, jnp.broadcast_to(col, diag.shape), 0.0), axis=0, keepdims=True))
+            packed.append(jnp.zeros((STAT - len(packed), LANES), F32))
+            acc[n, k, core, h, ur:ur + STAT, :] = jnp.concatenate(packed, axis=0)
+        pair(k, n).start()
 
     def column(stat):
         return jnp.sum(jnp.where(diag, jnp.broadcast_to(stat, diag.shape), 0.0), axis=1, keepdims=True)
@@ -304,29 +312,47 @@
 
     def sends(send, recv, ssem, rsem, devs):
         return [[remote(send.at[n, i], recv.at[n, i], ssem.at[n * AWAY + i], rsem.at[n * AWAY + i], devs[d])
-                 for i, d in enumerate((2, 1, -1))] for n in range(SPLITS)]
+                 for i, d in enumerate(HOPS[:AWAY])] for n in range(SPLITS)]
 
     xc = sends(xsend, xrecv, sem_xs, sem_xr, x_dev)
     yc = sends(ysend, yrecv, sem_ys, sem_yr, y_dev)
     oc = [remote(obuf.at[n, c], obuf.at[n, c], sem_os.at[n], sem_or.at[n], partner) for n in range(SPLITS)]
-    away = (FAR, RIGHT, LEFT)
 
     def both(n, k, h):
         return [acc.at[n, k, c, h], pbuf.at[n, k, h]]
 
-    def x_start(n):
-        for i, k in enumerate(away):
-            pair(k, n).wait_recv()
-            for h in range(2):
-                merge_into(xsend.at[n, i, h], both(n, k, h))
-            xc[n][i].start()
+    def x_start(n, k):
+        if k == OWN:
+            return
+        pair(k, n).wait_recv()
+        for h in range(2):
+            merge_into(xsend.at[n, k, h], both(n, k, h))
+        xc[n][k].start()
+
+    def fresh(n):
+        two = unit * kv
+        parity = iota((two, LANES), 0) % kv
+        for h in range(2):
+            rows16 = pl.ds(pl.multiple_of((((x * 2 + c) * SPLITS + n) * 2 + h) * two, two), two)
+            score_col = []
+            for core in range(kv):
+                k, v = [jnp.where(parity == core, r, pltpu.roll(r, 1 if core == 0 else two - 1, 0))
+                        for r in (kvq[i * n_w, rows16, :].astype(BF16).astype(F32) for i in range(2))]
+                for j in range(1, n_w):
+                    q = kvq[core * n_w + j, rows16, :].astype(BF16).astype(F32)
+                    score_col.append(jnp.sum(q * k, axis=1, keepdims=True) * fold)
+                    at = (core * (n_w - 1) + j - 1) * two
+                    newest[n, h, at:at + two, :] = v
+            col = jnp.broadcast_to(jnp.concatenate(score_col, axis=0), diag.shape)
+            peak = jnp.sum(jnp.where(diag, col, 0.0), axis=0, keepdims=True)
+            newest[n, h, ur:ur + STAT, :] = jnp.where(iota((STAT, LANES), 0) == 0, jnp.broadcast_to(peak, (STAT, LANES)), 1.0)
 
     def x_end(n):
         pair(OWN, n).wait_recv()
         for cp in xc[n]:
             cp.wait_recv()
         for h in range(2):
-            total, _, denom = merge(both(n, OWN, h) + [xrecv.at[n, i, h] for i in range(AWAY)])
+            total, _, denom = merge(both(n, OWN, h) + [newest.at[n, h]] + [xrecv.at[n, i, h] for i in range(AWAY)])
             obuf[n, c, h * ur:(h + 1) * ur, :] = (total / column(denom)).astype(BF16).astype(F32)
         oc[n].start()
 
@@ -344,8 +370,8 @@
                     head = (t * per + i) * LANES
                     lhs[n, at:at + unit, head:head + LANES] = obuf[
                         n, core, pl.ds(h * ur + t * unit * per + i, unit, stride=per), :]
-        for i, k in enumerate(away):
-            prod = product(n, k)
+        for i in range(AWAY):
+            prod = product(n, i)
             for h in range(2):
                 ysend[n, i, h] = prod[:, h * hc:(h + 1) * hc]
             yc[n][i].start()
@@ -473,10 +499,21 @@
                 take(n, fd, sd)
             s_end(n, 2)
 
-    attend(0)
-    x_start(0)
-    attend(1)
-    x_start(1)
+    scores = (score_a, score_b)
+    steps = [(n, k) for n in range(SPLITS) for k in range(ROUTES)]
+    score(*steps[0], scores[0])
+    for i, step in enumerate(steps):
+        if i + 1 < len(steps):
+            score(*steps[i + 1], scores[(i + 1) % 2])
+        finish(*step, scores[i % 2])
+        if i >= LAG:
+            x_start(*steps[i - LAG])
+    for step in steps[-LAG:]:
+        x_start(*step)
+    new_arrived()
+    for n in range(SPLITS):
+        fresh(n)
+    new_tokens()
     x_end(0)
     y_start(0)
     x_end(1)
@@ -523,6 +560,7 @@
         rows = batch // nx
         cols = d_model // (2 * tp)
         ur = batch // (sp * SPLITS * 2) * heads
+        scored = buf((batch // (ROUTES * SPLITS * GROUP), GROUP * heads, GROUP * seq_block * kv), F32)
         travel = buf((SPLITS, AWAY, 2, ur + STAT, head_dim), F32)
         yblock = buf((SPLITS, AWAY, 2, rows // SPLITS, cols // 2), F32)
         n_x, n_f = SPLITS * AWAY, SPLITS * ROUTES
@@ -542,6 +580,8 @@
                 buf((batch, d_model), BF16),
                 buf((n_w, d_model, BLOCK), BF16),
                 *dma((), (), (HID,), (n_w,), (PIECES,), (PIECES,), (n_w,), (n_w,)),
+                scored, scored,
+                buf((SPLITS, 2, ur + STAT, head_dim), F32),
                 buf((SPLITS, ROUTES, 2, 2, ur + STAT, head_dim), F32),
                 buf((SPLITS, ROUTES, 2, ur + STAT, head_dim), F32),
                 travel, travel,

time: 66.5 us -> 63.9 us (0.961)
  Pallas kernels: 65.8 us -> 63.2 us
    pallas_call x1, Pallas kernels: 61.5 us -> 58.8 us  [local_step(): pl.pallas_call(functools.partial(decode_kernel, seq_block, kv, heads), ou...]
where the time goes in v4:
time: 63.9 us; the launch traced here: 63.8 us
  Pallas kernels  63.2 us (99%)
  between operations  0.64 us (1%)
    pallas_call x1, Pallas kernels, local_step(): pl.pallas_call(functools.partial(decode_kernel, seq_block, kv, heads), ou...  58.8 us
    pallas_call x1, Pallas kernels, local_step(): pl.pallas_call(store_kernel, out_shape=tuple((shape(r.shape, r.dtype) for...  4.33 us

profile of v4, /device:TPU:97, one launch (start us, length us, event | category | flops | bytes accessed | tf_op | source)
XLA Modules:
  0.0 63.8 jit_solution(9899758941415745825)
XLA Ops:
  0.6 58.8 %decode_step.1 = (bf16[16384,128]{1,0:T(8,128)(2,1)S(1)}, bf16[16384,128]{1,0:T(8,128)(2,1)S(1)}, bf16[256,6144]{1,0:T(8,128)(2,1)S(1)}) custom-call(s32[256]{0:T(256)} %refs_0_.1, bf16[256,6144]{1,0:T(8,128)(2,1)} %refs_1_.1, bf16[6144]{0:T(1024)(128)(2,1)} %refs_2_.1, bf16[6144,1536]{1,0:T(8,128)(2,1)} %refs_3_.1, bf16[6144,256]{1,0:T(8,128)(2,1)} %refs_4_.1, ...), custom_call_target="tpu_custom_call" | custom-call | tf_op jit(solution)/shard_map/decode_step/pallas_call | solution.py:569
  59.5 4.3 %store.1 = (bf16[16384,128]{1,0:T(8,128)(2,1)}, bf16[16384,128]{1,0:T(8,128)(2,1)}, bf16[256,6144]{1,0:T(8,128)(2,1)}) custom-call(bf16[16384,128]{1,0:T(8,128)(2,1)S(1)} %get-tuple-element.9.refs_0_, bf16[16384,128]{1,0:T(8,128)(2,1)S(1)} %get-tuple-element.10.refs_1_, bf16[256,6144]{1,0:T(8,128)(2,1)S(1)} %get-tuple-element.11.refs_2_), custom_call_target="tpu_custom_call" | custom-call | tf_op jit(solution)/shard_map/store/pallas_call | solution.py:601

commit v5 on v4

--- a/solution.py
+++ b/solution.py
@@ -75,16 +75,16 @@
 
     def cache_copies(p):
         part = pl.ds(pl.multiple_of(p * crow, crow), crow)
-        return [pltpu.make_async_copy(src.at[part], buf.at[part], sem.at[p])
+        return [pltpu.make_async_copy(src.at[part], buf.at[part], sem)
                 for src, buf, sem in ((kc_hbm, kbuf, sem_k), (vc_hbm, vbuf, sem_v))]
 
     def trade(j):
         slot = kvq.at[c * n_w + j]
-        return remote(slot, slot, sem_s.at[j], sem_r.at[j], partner)
+        return remote(slot, slot, sem_s, sem_r.at[j], partner)
 
     def arrival(j):
         slot = kvq.at[(1 - c) * n_w + j]
-        return remote(slot, slot, sem_s.at[j], sem_r.at[j], partner)
+        return remote(slot, slot, sem_s, sem_r.at[j], partner)
 
     for cp in hid_copies + [gain_copy, len_copy]:
         cp.start()
@@ -125,7 +125,7 @@
                 q_copy(i + 1).start()
             else:
                 kv_start()
-        lax.fori_loop(i * rows_h // step, (i + 1) * rows_h // step, norm_rows, 0)
+        lax.fori_loop(i * rows_h // step, (i + 1) * rows_h // step, norm_rows, 0, unroll=True)
     enter()
 
     per_step = PIECES // n_w
@@ -149,9 +149,8 @@
     lax.fori_loop(0, n_w, columns, 0)
     trade(0).start()
     len_copy.wait()
-    for p in range(PIECES):
-        for cp in cache_copies(p):
-            cp.wait()
+    for src, buf, sem in ((kc_hbm, kbuf, sem_k), (vc_hbm, vbuf, sem_v)):
+        pltpu.make_async_copy(src, buf, sem).wait()
     for j in range(1, n_w):
         arrival(j).wait_recv()
 
@@ -173,8 +172,8 @@
 
     def new_tokens():
         lax.fori_loop(0, PIECES, update, 0)
-        for j in range(n_w):
-            trade(j).wait_send()
+        sent = kvq.at[pl.ds(c * n_w, n_w)]
+        remote(sent, sent, sem_s, sem_r.at[0], partner).wait_send()
 
     return arrival(0).wait_recv, new_tokens
 
@@ -253,7 +252,7 @@
     groups = [(core, h, g) for core, h in halves for g in range(unit // GROUP)]
 
     def pair(k, n):
-        return remote(acc.at[n, k, 1 - c], pbuf.at[n, k], sem_ps.at[n * ROUTES + k], sem_pr.at[n * ROUTES + k], partner)
+        return remote(acc.at[n, k, 1 - c], pbuf.at[n, k], sem_ps.at[n], sem_pr.at[n * ROUTES + k], partner)
 
     def first(n, k, core, h, g):
         dest = at_x(HOPS[k])
@@ -311,7 +310,7 @@
         dst[ur:ur + STAT, :] = jnp.concatenate([peak, denom, jnp.zeros((STAT - 2, LANES), F32)], axis=0)
 
     def sends(send, recv, ssem, rsem, devs):
-        return [[remote(send.at[n, i], recv.at[n, i], ssem.at[n * AWAY + i], rsem.at[n * AWAY + i], devs[d])
+        return [[remote(send.at[n, i], recv.at[n, i], ssem.at[n], rsem.at[n * AWAY + i], devs[d])
                  for i, d in enumerate(HOPS[:AWAY])] for n in range(SPLITS)]
 
     xc = sends(xsend, xrecv, sem_xs, sem_xr, x_dev)
@@ -378,11 +377,8 @@
 
     f = x + c * (y - x)
     s = y + c * (x - y)
-    sent = []
-
     def go(copy):
         copy.start()
-        sent.append(copy)
 
     def f_dev(d):
         return {'tp': (y + c * d + ny) % ny, 'sp': ((x + (1 - c) * d + nx) % nx) * 2 + c}
@@ -402,14 +398,14 @@
             ref = ref.at[0 if d > 0 else 1]
         if ring == 'f':
             i = n * ROUTES + kind(d, is_half)
-            return remote(ref, ref, sem_fs.at[i], sem_fr.at[i], f_dev(d))
+            return remote(ref, ref, sem_fs.at[n], sem_fr.at[i], f_dev(d))
         i = (n * nx + fd % nx) * ROUTES + kind(d, is_half)
-        return remote(ref, ref, sem_ss.at[i], sem_sr.at[i], s_dev(d))
+        return remote(ref, ref, sem_ss.at[n], sem_sr.at[i], s_dev(d))
 
     def over(n, fd, sd):
         i = (n * nx + fd % nx) * ny + sd % ny
         ref = block(n, fd, sd)
-        return remote(ref, ref, sem_ds.at[i], sem_dr.at[i], partner)
+        return remote(ref, ref, sem_ds.at[n], sem_dr.at[i], partner)
 
     def place(n, ci, fi, si, swap):
         xi, yi = fi + swap * (si - fi), si + swap * (fi - si)
@@ -476,7 +472,7 @@
         i = (n * nx + fd % nx) * ny + sd % ny
         fi, si = (s + fd + nx) % nx, (f + sd + ny) % ny
         ref = gbuf.at[n, 1 - c, fi, si]
-        remote(ref, ref, sem_ds.at[i], sem_dr.at[i], partner).wait_recv()
+        remote(ref, ref, sem_ds.at[n], sem_dr.at[i], partner).wait_recv()
         place(n, 1 - c, fi, si, 1 - c)
 
     def stage(n, i):
@@ -527,13 +523,10 @@
         for fd, sd in ((2, -1), (2, 1), (-1, 2), (1, 2), (2, 2)):
             take(n, fd, sd)
     for n in range(SPLITS):
-        for k in range(ROUTES):
-            pair(k, n).wait_send()
-    for cp in xc + yc:
-        for one in cp:
-            one.wait_send()
-    for cp in oc + sent:
-        cp.wait_send()
+        done = ((acc.at[n, :, 1 - c], sem_ps), (xsend.at[n], sem_xs), (obuf.at[n, c], sem_os), (ysend.at[n], sem_ys),
+                (gbuf.at[n, c, 0, pl.ds(0, AWAY)], sem_fs), (gbuf.at[n, c, pl.ds(0, AWAY)], sem_ss), (gbuf.at[n, c], sem_ds))
+        for ref, sem in done:
+            remote(ref, ref, sem.at[n], sem_or.at[n], partner).wait_send()
 
 
 def solution(mesh):
@@ -566,6 +559,7 @@
         n_x, n_f = SPLITS * AWAY, SPLITS * ROUTES
         n_s = n_f * nx
         n_d = SPLITS * nx * tp
+        split = (SPLITS,)
         k_new, v_new, out = pl.pallas_call(
             functools.partial(decode_kernel, seq_block, kv, heads),
             out_shape=(buf((flat, head_dim), BF16), buf((flat, head_dim), BF16), buf((batch, d_model), BF16)),
@@ -579,7 +573,7 @@
                 buf((1, d_model), F32),
                 buf((batch, d_model), BF16),
                 buf((n_w, d_model, BLOCK), BF16),
-                *dma((), (), (HID,), (n_w,), (PIECES,), (PIECES,), (n_w,), (n_w,)),
+                *dma((), (), (HID,), (n_w,), (), (), (), (n_w,)),
                 scored, scored,
                 buf((SPLITS, 2, ur + STAT, head_dim), F32),
                 buf((SPLITS, ROUTES, 2, 2, ur + STAT, head_dim), F32),
@@ -590,8 +584,8 @@
                 buf((ROUTES, width, cols), BF16),
                 yblock, yblock,
                 buf((SPLITS, 2, nx, tp, 2, rows // SPLITS, cols // 2), F32),
-                *dma((ROUTES,), (n_f,), (n_f,), (n_x,), (n_x,), (SPLITS,), (SPLITS,), (n_x,), (n_x,),
-                     (n_f,), (n_f,), (n_s,), (n_s,), (n_d,), (n_d,)),
+                *dma((ROUTES,), split, (n_f,), split, (n_x,), split, split, split, (n_x,),
+                     split, (n_f,), split, (n_s,), split, (n_d,)),
             ],
             compiler_params=pltpu.CompilerParams(collective_id=0, has_side_effects=True, vmem_limit_bytes=VMEM_MIB * MIB),
             name='decode_step',

time: 63.9 us -> 62.5 us (0.978)
  Pallas kernels: 63.2 us -> 61.8 us
    pallas_call x1, Pallas kernels: 58.8 us -> 57.4 us  [local_step(): pl.pallas_call(functools.partial(decode_kernel, seq_block, kv, heads), ou...]
where the time goes in v5:
time: 62.5 us; the launch traced here: 62.4 us
  Pallas kernels  61.8 us (99%)
  between operations  0.64 us (1%)
    pallas_call x1, Pallas kernels, local_step(): pl.pallas_call(functools.partial(decode_kernel, seq_block, kv, heads), ou...  57.4 us
    pallas_call x1, Pallas kernels, local_step(): pl.pallas_call(store_kernel, out_shape=tuple((shape(r.shape, r.dtype) for...  4.33 us

profile of v5, /device:TPU:97, one launch (start us, length us, event | category | flops | bytes accessed | tf_op | source)
XLA Modules:
  0.0 62.4 jit_solution(17171874994742718107)
XLA Ops:
  0.6 57.4 %decode_step.1 = (bf16[16384,128]{1,0:T(8,128)(2,1)S(1)}, bf16[16384,128]{1,0:T(8,128)(2,1)S(1)}, bf16[256,6144]{1,0:T(8,128)(2,1)S(1)}) custom-call(s32[256]{0:T(256)} %refs_0_.1, bf16[256,6144]{1,0:T(8,128)(2,1)} %refs_1_.1, bf16[6144]{0:T(1024)(128)(2,1)} %refs_2_.1, bf16[6144,1536]{1,0:T(8,128)(2,1)} %refs_3_.1, bf16[6144,256]{1,0:T(8,128)(2,1)} %refs_4_.1, ...), custom_call_target="tpu_custom_call" | custom-call | tf_op jit(solution)/shard_map/decode_step/pallas_call | solution.py:563
  58.1 4.3 %store.1 = (bf16[16384,128]{1,0:T(8,128)(2,1)}, bf16[16384,128]{1,0:T(8,128)(2,1)}, bf16[256,6144]{1,0:T(8,128)(2,1)}) custom-call(bf16[16384,128]{1,0:T(8,128)(2,1)S(1)} %get-tuple-element.9.refs_0_, bf16[16384,128]{1,0:T(8,128)(2,1)S(1)} %get-tuple-element.10.refs_1_, bf16[256,6144]{1,0:T(8,128)(2,1)S(1)} %get-tuple-element.11.refs_2_), custom_call_target="tpu_custom_call" | custom-call | tf_op jit(solution)/shard_map/store/pallas_call | solution.py:595

commit v6 on v5

--- a/solution.py
+++ b/solution.py
@@ -25,6 +25,8 @@
 HID = 4
 FAR, RIGHT, LEFT, OWN = range(4)
 HOPS = (2, 1, -1, 0)
+ONE_HOP_F = ()
+ONE_HOP_S = ((1, 2),)
 LAG = 3
 AWAY = 3
 ROUTES = 4
@@ -390,7 +392,7 @@
         return gbuf.at[n, c, (f + fd + nx) % nx, (s + sd + ny) % ny]
 
     def kind(d, is_half):
-        return is_half * 2 + (d > 0)
+        return 2 if d == 2 else is_half * 2 + (d > 0)
 
     def along(ring, n, fd, sd, d, is_half=False):
         ref = block(n, fd, sd)
@@ -419,7 +421,7 @@
         place(n, c, (f + fd + nx) % nx, (s + sd + ny) % ny, c)
 
     def spread(n, fd):
-        for d in (1, -1):
+        for d in HOPS[:AWAY] if (n, fd) in ONE_HOP_S else (1, -1):
             go(along('s', n, fd, 0, d))
         go(over(n, fd, 0))
 
@@ -433,38 +435,44 @@
             kept = jnp.concatenate([hbuf[pl.ds(pl.multiple_of(x * rows + (core * SPLITS + n) * part, part), part), at]
                                     for core in range(2)], axis=0)
             gbuf[n, c, f, s, h] = (kept.astype(F32) + total).astype(BF16).astype(F32)
-        for d in (1, -1):
+        for d in (1, -1, 2) if n in ONE_HOP_F else (1, -1):
             go(along('f', n, 0, 0, d))
         spread(n, 0)
         place_here(n, 0, 0)
 
-    def pass_on(ring, n, fd, sd, d):
-        along(ring, n, fd, sd, d).wait_recv()
-        go(along(ring, n, fd, sd, d, True))
-
     def f_ring(n):
         for d in (1, -1):
-            pass_on('f', n, -d, 0, d)
+            along('f', n, -d, 0, d).wait_recv()
+            if n not in ONE_HOP_F:
+                go(along('f', n, -d, 0, d, True))
             spread(n, -d)
         for d in (1, -1):
             place_here(n, -d, 0)
 
     def f_end(n):
-        for d in (1, -1):
-            along('f', n, 2, 0, d, True).wait_recv()
+        if n in ONE_HOP_F:
+            along('f', n, 2, 0, 2).wait_recv()
+        else:
+            for d in (1, -1):
+                along('f', n, 2, 0, d, True).wait_recv()
         spread(n, 2)
         place_here(n, 2, 0)
 
     def s_ring(n, fd):
         for d in (1, -1):
-            pass_on('s', n, fd, -d, d)
+            along('s', n, fd, -d, d).wait_recv()
+            if (n, fd) not in ONE_HOP_S:
+                go(along('s', n, fd, -d, d, True))
             go(over(n, fd, -d))
         for d in (1, -1):
             place_here(n, fd, -d)
 
     def s_end(n, fd):
-        for d in (1, -1):
-            along('s', n, fd, 2, d, True).wait_recv()
+        if (n, fd) in ONE_HOP_S:
+            along('s', n, fd, 2, 2).wait_recv()
+        else:
+            for d in (1, -1):
+                along('s', n, fd, 2, d, True).wait_recv()
         go(over(n, fd, 2))
         place_here(n, fd, 2)
 

time: 62.5 us -> 61.9 us (level)
  Pallas kernels: 61.8 us -> 61.1 us
    pallas_call x1, Pallas kernels: 57.4 us -> 56.8 us  [local_step(): pl.pallas_call(functools.partial(decode_kernel, seq_block, kv, heads), ou...]
where the time goes in v6:
time: 61.9 us; the launch traced here: 61.8 us
  Pallas kernels  61.1 us (99%)
  between operations  0.64 us (1%)
    pallas_call x1, Pallas kernels, local_step(): pl.pallas_call(functools.partial(decode_kernel, seq_block, kv, heads), ou...  56.8 us
    pallas_call x1, Pallas kernels, local_step(): pl.pallas_call(store_kernel, out_shape=tuple((shape(r.shape, r.dtype) for...  4.33 us

profile of v6, /device:TPU:97, one launch (start us, length us, event | category | flops | bytes accessed | tf_op | source)
XLA Modules:
  0.0 61.8 jit_solution(8801502723864308628)
XLA Ops:
  0.6 56.8 %decode_step.1 = (bf16[16384,128]{1,0:T(8,128)(2,1)S(1)}, bf16[16384,128]{1,0:T(8,128)(2,1)S(1)}, bf16[256,6144]{1,0:T(8,128)(2,1)S(1)}) custom-call(s32[256]{0:T(256)} %refs_0_.1, bf16[256,6144]{1,0:T(8,128)(2,1)} %refs_1_.1, bf16[6144]{0:T(1024)(128)(2,1)} %refs_2_.1, bf16[6144,1536]{1,0:T(8,128)(2,1)} %refs_3_.1, bf16[6144,256]{1,0:T(8,128)(2,1)} %refs_4_.1, ...), custom_call_target="tpu_custom_call" | custom-call | tf_op jit(solution)/shard_map/decode_step/pallas_call | solution.py:571
  57.4 4.3 %store.1 = (bf16[16384,128]{1,0:T(8,128)(2,1)}, bf16[16384,128]{1,0:T(8,128)(2,1)}, bf16[256,6144]{1,0:T(8,128)(2,1)}) custom-call(bf16[16384,128]{1,0:T(8,128)(2,1)S(1)} %get-tuple-element.9.refs_0_, bf16[16384,128]{1,0:T(8,128)(2,1)S(1)} %get-tuple-element.10.refs_1_, bf16[256,6144]{1,0:T(8,128)(2,1)S(1)} %get-tuple-element.11.refs_2_), custom_call_target="tpu_custom_call" | custom-call | tf_op jit(solution)/shard_map/store/pallas_call | solution.py:603

commit v7 on v6

--- a/solution.py
+++ b/solution.py
@@ -23,8 +23,8 @@
 SPLITS = 2
 PIECES = 16
 HID = 4
-FAR, RIGHT, LEFT, OWN = range(4)
-HOPS = (2, 1, -1, 0)
+OWN = 3
+HOPS = (1, 2, -1, 0)
 ONE_HOP_F = ()
 ONE_HOP_S = ((1, 2),)
 LAG = 3

time: 61.9 us -> 61.3 us (level)
  no operation moved by 1% of the time
where the time goes in v7:
time: 61.3 us; the launch traced here: 61.1 us
  Pallas kernels  60.5 us (99%)
  between operations  0.64 us (1%)
    pallas_call x1, Pallas kernels, local_step(): pl.pallas_call(functools.partial(decode_kernel, seq_block, kv, heads), ou...  56.2 us
    pallas_call x1, Pallas kernels, local_step(): pl.pallas_call(store_kernel, out_shape=tuple((shape(r.shape, r.dtype) for...  4.33 us

profile of v7, /device:TPU:97, one launch (start us, length us, event | category | flops | bytes accessed | tf_op | source)
XLA Modules:
  0.0 61.1 jit_solution(9364500915881820727)
XLA Ops:
  0.6 56.2 %decode_step.1 = (bf16[16384,128]{1,0:T(8,128)(2,1)S(1)}, bf16[16384,128]{1,0:T(8,128)(2,1)S(1)}, bf16[256,6144]{1,0:T(8,128)(2,1)S(1)}) custom-call(s32[256]{0:T(256)} %refs_0_.1, bf16[256,6144]{1,0:T(8,128)(2,1)} %refs_1_.1, bf16[6144]{0:T(1024)(128)(2,1)} %refs_2_.1, bf16[6144,1536]{1,0:T(8,128)(2,1)} %refs_3_.1, bf16[6144,256]{1,0:T(8,128)(2,1)} %refs_4_.1, ...), custom_call_target="tpu_custom_call" | custom-call | tf_op jit(solution)/shard_map/decode_step/pallas_call | solution.py:571
  56.8 4.3 %store.1 = (bf16[16384,128]{1,0:T(8,128)(2,1)}, bf16[16384,128]{1,0:T(8,128)(2,1)}, bf16[256,6144]{1,0:T(8,128)(2,1)}) custom-call(bf16[16384,128]{1,0:T(8,128)(2,1)S(1)} %get-tuple-element.9.refs_0_, bf16[16384,128]{1,0:T(8,128)(2,1)S(1)} %get-tuple-element.10.refs_1_, bf16[256,6144]{1,0:T(8,128)(2,1)S(1)} %get-tuple-element.11.refs_2_), custom_call_target="tpu_custom_call" | custom-call | tf_op jit(solution)/shard_map/store/pallas_call | solution.py:603

commit v8 on v7

--- a/solution.py
+++ b/solution.py
@@ -135,9 +135,11 @@
     def columns(it, carry):
         j = (it + 1) % n_w
         w_copy(j, wk_hbm, 0).wait()
-        for i in range(per_step):
-            for cp in cache_copies(it * per_step + i):
-                cp.start()
+        @pl.when(it < 2)
+        def _():
+            for i in range(2 * per_step):
+                for cp in cache_copies(it * 2 * per_step + i):
+                    cp.start()
 
         @pl.when(it > 0)
         def _():

time: 61.3 us -> 61.2 us (level)
  no operation moved by 1% of the time
where the time goes in v8:
time: 61.2 us; the launch traced here: 61.1 us
  Pallas kernels  60.5 us (99%)
  between operations  0.64 us (1%)
    pallas_call x1, Pallas kernels, local_step(): pl.pallas_call(functools.partial(decode_kernel, seq_block, kv, heads), ou...  56.1 us
    pallas_call x1, Pallas kernels, local_step(): pl.pallas_call(store_kernel, out_shape=tuple((shape(r.shape, r.dtype) for...  4.33 us

profile of v8, /device:TPU:97, one launch (start us, length us, event | category | flops | bytes accessed | tf_op | source)
XLA Modules:
  0.0 61.1 jit_solution(11452740212597351750)
XLA Ops:
  0.6 56.1 %decode_step.1 = (bf16[16384,128]{1,0:T(8,128)(2,1)S(1)}, bf16[16384,128]{1,0:T(8,128)(2,1)S(1)}, bf16[256,6144]{1,0:T(8,128)(2,1)S(1)}) custom-call(s32[256]{0:T(256)} %refs_0_.1, bf16[256,6144]{1,0:T(8,128)(2,1)} %refs_1_.1, bf16[6144]{0:T(1024)(128)(2,1)} %refs_2_.1, bf16[6144,1536]{1,0:T(8,128)(2,1)} %refs_3_.1, bf16[6144,256]{1,0:T(8,128)(2,1)} %refs_4_.1, ...), custom_call_target="tpu_custom_call" | custom-call | tf_op jit(solution)/shard_map/decode_step/pallas_call | solution.py:573
  56.8 4.3 %store.1 = (bf16[16384,128]{1,0:T(8,128)(2,1)}, bf16[16384,128]{1,0:T(8,128)(2,1)}, bf16[256,6144]{1,0:T(8,128)(2,1)}) custom-call(bf16[16384,128]{1,0:T(8,128)(2,1)S(1)} %get-tuple-element.9.refs_0_, bf16[16384,128]{1,0:T(8,128)(2,1)S(1)} %get-tuple-element.10.refs_1_, bf16[256,6144]{1,0:T(8,128)(2,1)S(1)} %get-tuple-element.11.refs_2_), custom_call_target="tpu_custom_call" | custom-call | tf_op jit(solution)/shard_map/store/pallas_call | solution.py:605
